TPU v7x, 256 devices: a whole 4x4x8 slice. The times are simulated.
256 devices in a mesh: feat: 64 (over y, z, core), samp: 4 (over x).
Axes of the slice: x: 4, y: 4, z: 8, core: 2. Of those that a mesh axis runs over, the one named last changes fastest.
Arguments:
- design: bfloat16 [14336, 65536], P('samp', 'feat'), may hold values from -0.125 to 0.125
- targets: bfloat16 [14336, 128], P('samp'), may hold values from -26 to 26
- warm_start: float32 [65536, 128], P('feat'), may hold values from -0.6 to 0.6
- active_mask: int32 [2, 65536], P(None, 'feat'), may hold values 0 or 1
- penalty_index: int32 [1], replicated, may hold values from 0 to 7
Outputs:
- coefficients: float32 [65536, 128], P('feat')
- correlations: float32 [3, 65536], P(None, 'feat')
- relative_gaps: float32 [3], replicated
- pruned_counts: float32 [2], replicated
All inputs are finite; a program needn't handle non-finite values. No bound on the sum of `active_mask` on one device may be relied on, other than what follows from the above.
Results may differ from a plain program's by a relative error of at most 0.0024.
The roundings to bfloat16 on the way count: a program that leaves them out, or rounds other values in their place, can miss the bound.
Values may be sent and summed in bfloat16 or wider, within the bound.
No kernel may reach another device: no remote copies, remote signals or barrier semaphores. Data moves between devices by JAX's collectives and lax.ppermute only.
A program may use at most 64 MiB of HBM per device.

v0:
```python
import jax
import jax.numpy as jnp
from jax import lax
from jax.experimental import pallas as pl
from jax.experimental.pallas import tpu as pltpu
from jax.sharding import Mesh
from jax.sharding import PartitionSpec as P


ITERS = 2
FEAT = ("y", "z", "core")
PLANE = ("y", "z")
BF = jnp.bfloat16
F32 = jnp.float32
EXTRA = 8
VMEM = pl.BlockSpec(memory_space=pltpu.VMEM)
SMEM = pl.BlockSpec(memory_space=pltpu.SMEM)


def shape_of(dims, dtype=F32):
    return jax.ShapeDtypeStruct(tuple(dims), dtype)


def call(body, outs, *args, smem=(), smem_outs=(), scratch=(), mib=4):
    single = not isinstance(outs, (list, tuple))
    shapes = [outs] if single else list(outs)
    out_specs = [SMEM if k in smem_outs else VMEM for k in range(len(shapes))]
    return pl.pallas_call(
        body,
        out_shape=shapes[0] if single else tuple(shapes),
        in_specs=[SMEM if k in smem else VMEM for k in range(len(args))],
        out_specs=out_specs[0] if single else tuple(out_specs),
        scratch_shapes=list(scratch),
        compiler_params=pltpu.CompilerParams(vmem_limit_bytes=mib << 20),
    )(*args)


def shifted(value, axis, by):
    n = lax.axis_size(axis)
    return lax.ppermute(value, axis, [(i, (i + by) % n) for i in range(n)])


def lane(row, index, value):
    at = lax.broadcasted_iota(jnp.int32, row.shape, 1)
    return jnp.where(at == index, value, row)


def lane_norms(value):
    return jnp.sqrt(jnp.sum(value * value, axis=0, keepdims=True))


def in_hbm(value):
    return pltpu.with_memory_space_constraint(value, pltpu.HBM)


def half_start(near, half):
    core = lax.axis_index("core")
    return (core if near else 1 - core) * half


def block_at(k, width):
    return pl.multiple_of(((lax.axis_index("samp") + k) & 3) * width, width)


def corr_first(design, targets, step, block):
    rows, cols = design.shape
    tasks = targets.shape[1]
    width = cols // 4
    count = rows // step

    def body(design, targets, o0, o1, o2, o3, held, own, right, total, squares, arrived):
        plane = lax.axis_index("y") * lax.axis_size("z") + lax.axis_index("z")
        at = pl.multiple_of(half_start(True, rows // 2) + plane * block, 8)
        mine = pltpu.make_async_copy(targets.at[pl.ds(at, block)], own, arrived.at[2 * count])

        def pieces(i):
            here = pl.ds(pl.multiple_of(i * step, step), step)
            return (
                pltpu.make_async_copy(targets.at[here], right.at[here], arrived.at[2 * i]),
                pltpu.make_async_copy(design.at[here], held.at[here], arrived.at[2 * i + 1]),
            )

        for i in range(count):
            for piece in pieces(i):
                piece.start()
        mine.start()
        total[...] = jnp.zeros_like(total)
        squares[...] = jnp.zeros_like(squares)

        def one(i, carry):
            for piece in pieces(i):
                piece.wait()
            here = pl.ds(pl.multiple_of(i * step, step), step)
            total[...] += turned_dot(right[here, :], held[here, :])

            def part(j, carry):
                inner = pl.multiple_of(i * step + j * 64, 64)
                wide = held[pl.ds(inner, 64), :].astype(F32)
                squares[...] += jnp.sum((wide * wide).reshape(8, 8, cols), axis=0)
                return carry

            lax.fori_loop(0, step // 64, part, 0)
            return carry

        lax.fori_loop(0, count, one, 0)
        mine.wait()
        for k, out in enumerate((o0, o1, o2, o3)):
            at = block_at(k, width)
            out[:tasks, :] = total[:, pl.ds(at, width)]
            out[tasks:, :] = squares[:, pl.ds(at, width)]

    hbm = pl.BlockSpec(memory_space=pltpu.HBM)
    return pl.pallas_call(
        body,
        out_shape=(
            *[shape_of((tasks + 8, width))] * 4,
            pltpu.VMEM(design.shape, design.dtype),
            shape_of((block, tasks), targets.dtype),
        ),
        in_specs=[hbm, hbm],
        out_specs=(VMEM,) * 6,
        scratch_shapes=[
            pltpu.VMEM((rows, tasks), targets.dtype),
            pltpu.VMEM((tasks, cols), F32),
            pltpu.VMEM((8, cols), F32),
            pltpu.SemaphoreType.DMA((2 * count + 1,)),
        ],
        compiler_params=pltpu.CompilerParams(vmem_limit_bytes=16 << 20),
        name="corr_first",
    )(in_hbm(design), in_hbm(targets))


def fit_warm(near, design, warm, rows, step):
    cols, tasks = warm.shape
    width = cols // 4

    def body(design, warm, out, *turned):
        right = warm[...].astype(BF)
        if near:
            turned[0][...] = warm[pl.ds(block_at(0, width), width), :].T

        def one(i, carry):
            at = pl.multiple_of(half_start(near, rows) + i * step, step)
            out[pl.ds(pl.multiple_of(i * step, step), step), :] = jnp.dot(
                design[pl.ds(at, step), :], right, preferred_element_type=F32
            )
            return carry

        lax.fori_loop(0, rows // step, one, 0)

    outs = [shape_of((rows, tasks))] + ([shape_of((tasks, width))] if near else [])
    return call(body, outs, design, warm)


def fit_rows(near, design, blocks, rows, step):
    tasks, width = blocks[0].shape

    def body(design, c0, c1, c2, c3, out, whole):
        for k, block in enumerate((c0, c1, c2, c3)):
            whole[:, pl.ds(block_at(k, width), width)] = block[...].astype(BF)

        def one(i, carry):
            at = pl.multiple_of(half_start(near, rows) + i * step, step)
            out[pl.ds(pl.multiple_of(i * step, step), step), :] = lax.dot_general(
                design[pl.ds(at, step), :],
                whole[...],
                (((1,), (1,)), ((), ())),
                preferred_element_type=F32,
            )
            return carry

        lax.fori_loop(0, rows // step, one, 0)

    return call(
        body, shape_of((rows, tasks)), design, *blocks,
        scratch=[pltpu.VMEM((tasks, 4 * width), BF)],
    )


def joined(near, arrived, planes, corr=None):
    rows, tasks = near.shape
    outs = [shape_of((planes, rows // planes, tasks), BF)]
    if corr:
        outs += [shape_of((1, corr[0].shape[1])), shape_of((EXTRA, tasks))]

    def body(near, arrived, *refs):
        out = refs[len(corr)] if corr else refs[0]
        total = near[...] + arrived[...]
        out[...] = total.reshape(out.shape).astype(BF)
        if corr:
            c0, c1, c2, c3, _, steps, top = refs
            both = c0[...] + c1[...] + c2[...] + c3[...]
            column_squares = jnp.sum(both[tasks:], axis=0, keepdims=True)
            steps[...] = 0.5 / (1.0 + column_squares)
            top[...] = jnp.full(top.shape, jnp.max(lane_norms(both[:tasks])), F32)

    return call(body, outs, near, arrived, *(corr or []))


def turned_dot(right, left):
    return lax.dot_general(right, left, (((0,), (0,)), ((), ())), preferred_element_type=F32)


def grad_loop(near, right, design, total, block):
    planes = right.shape[0]
    group = 8
    step = group * block

    def one(i, carry):
        rows = right[pl.ds(i * group, group)].astype(F32)[:, :block]
        rows = rows.reshape(step, right.shape[2]).astype(BF)
        at = pl.multiple_of(half_start(near, planes * block) + i * step, step)
        total[...] += turned_dot(rows, design[pl.ds(at, step), :])
        return carry

    lax.fori_loop(0, planes // group, one, 0)


def grad_near(design, right, block):
    def body(design, right, total):
        total[...] = jnp.zeros_like(total)
        grad_loop(True, right, design, total, block)

    out = shape_of((right.shape[2], design.shape[1]))
    return call(body, out, design, right)


def top_of(right, block):
    pieces = right[:, block:, :].astype(F32)
    return jnp.max(jnp.sum(pieces, axis=1))


def grad_far(design, right, start, block, near=None):
    tasks, cols = start.shape
    width = cols // 4
    extra = 0 if near is None else EXTRA

    def body(design, right, start, *refs):
        outs, total = refs[-5:-1], refs[-1]
        total[...] = start[...]
        grad_loop(False, right, design, total, block)
        for k, out in enumerate(outs):
            at = block_at(k, width)
            out[:tasks, :] = total[:, pl.ds(at, width)]
        if extra:
            top = jnp.maximum(top_of(right, block), top_of(refs[0], block))
            for out in outs:
                out[tasks:, :] = jnp.full((extra, width), top, F32)

    outs = [shape_of((tasks + extra, width))] * 4
    args = [design, right, start] + ([] if near is None else [near])
    return call(body, outs, *args, scratch=[pltpu.VMEM((tasks, cols), F32)])


def residual_of(parts, own, at, stats=None, top=None):
    planes, block, tasks = parts.shape
    extra = 0 if top is None else EXTRA
    outs = [shape_of((planes, block + extra, tasks), BF), shape_of((1, 128))]

    def body(parts, own, given, copies, stats_out):
        fitted = jnp.sum(parts[...].astype(F32), axis=0)
        target = own[...].astype(F32)
        rounded = (target - fitted).astype(BF)
        wide = rounded.astype(F32)
        if extra:
            value = given[...]
            high = value.astype(BF).astype(F32)
            middle = (value - high).astype(BF).astype(F32)
            low = (value - high) - middle
            which = lax.broadcasted_iota(jnp.int32, value.shape, 0)
            tail = jnp.where(which == 0, high, jnp.where(which == 1, middle, low))
            tail = jnp.where(which < 3, tail, 0.0)
            rounded = jnp.concatenate([wide, tail], axis=0).astype(BF)
            row = jnp.zeros(stats_out.shape, F32)
        else:
            row = given[...]
        row = lane(row, at, jnp.sum(wide * wide))
        stats_out[...] = lane(row, at + 1, jnp.sum(wide * target))
        copies[...] = jnp.broadcast_to(rounded[None], copies.shape)

    return call(body, outs, parts, own, stats if top is None else top)


def penalty_of(top, index):
    return top / (8.0 + 4.0 * index[0].astype(F32))


def prox(parts, current, steps, mask, index, stats, at, out_dtype, tops=None):
    tasks, width = current.shape
    row_at = at // 8

    def body(own, r1, r2, r3, current, steps, mask, index, stats, *refs):
        new, sent, norms_out, stats_out, tops_out = refs[-5:]
        gradient = own[:tasks, :] + r1[:tasks, :] + r2[:tasks, :] + r3[:tasks, :]
        if tops is None:
            tops_out[...] = jnp.maximum(
                jnp.maximum(own[tasks:, :], r1[tasks:, :]),
                jnp.maximum(r2[tasks:, :], r3[tasks:, :]),
            )
        else:
            tops_out[...] = refs[0][...]
        norms = lane_norms(gradient)
        norms_out[...] = norms
        here = current[...]
        keep = mask[row_at : row_at + 1, pl.ds(block_at(0, width), width)].astype(F32)
        row = lane(stats[...], at + 2, jnp.sum(lane_norms(here)))
        row = lane(row, at + 3, jnp.max(norms))
        stats_out[...] = lane(row, at + 4, jnp.sum(1.0 - keep))
        penalty = penalty_of(tops_out[0:1, :], index)
        step = steps[...]
        moved = here + step * gradient
        moved_norms = lane_norms(moved)
        cutoff = step * penalty
        factor = jnp.maximum(moved_norms - cutoff, 0.0) / jnp.maximum(moved_norms, cutoff)
        value = (keep * factor) * moved
        new[...] = value
        sent[...] = value.astype(out_dtype)

    outs = [
        shape_of((tasks, width)),
        shape_of((tasks, width), out_dtype),
        shape_of((1, width)),
        shape_of(stats.shape),
        shape_of((EXTRA, width)),
    ]
    args = [*parts, current, steps, mask, index, stats] + ([] if tops is None else [tops])
    return call(body, outs, *args, smem=(7,))


def last_norms(parts, current, stats, n0, n1, at):
    width = n0.shape[1]

    def body(own, r1, r2, r3, current, stats, n0, n1, out):
        norms = lane_norms(own[...] + r1[...] + r2[...] + r3[...])
        row = lane(stats[...], at + 2, jnp.sum(lane_norms(current[...])))
        row = lane(row, at + 3, jnp.max(norms))
        wide = jnp.concatenate([row] * (width // row.shape[1]), axis=1)
        out[...] = jnp.concatenate([n0[...], n1[...], norms] + [wide] * 5, axis=0)

    return call(body, shape_of((8, width)), *parts, current, stats, n0, n1)


def of_samples(blocks, copies):
    def body(own, n1, n2, n3, out):
        rows = [ref[3:4, 0:128] for ref in (own, n1, n2, n3)]
        total = (rows[0] + rows[2]) + (rows[1] + rows[3])
        high = jnp.maximum(jnp.maximum(rows[0], rows[2]), jnp.maximum(rows[1], rows[3]))
        at = lax.broadcasted_iota(jnp.int32, total.shape, 1)
        out[...] = jnp.broadcast_to(jnp.where((at & 7) == 3, high, total), out.shape)

    return call(body, shape_of((copies, 128)), *blocks)


def finish(everyone, tops, index, blocks):
    width = blocks[0].shape[1]

    def body(everyone, tops, index, n0, n1, n2, n3, correlations, gaps, counts):
        values = everyone[...]
        sums = jnp.sum(values, axis=0, keepdims=True)
        highs = jnp.max(values, axis=0, keepdims=True)
        at_lane = lax.broadcasted_iota(jnp.int32, sums.shape, 1)

        def total(i):
            return jnp.full(sums.shape, jnp.sum(jnp.where(at_lane == i, sums, 0.0)), F32)

        penalty = penalty_of(tops[0:1, 0:128], index)
        row = jnp.zeros(sums.shape, F32)
        for t in range(ITERS + 1):
            at = 8 * t
            rr, ry, bn = total(at), total(at + 1), total(at + 2)
            top = jnp.max(jnp.where(at_lane == at + 3, highs, 0.0))
            scale = jnp.maximum(penalty, top)
            ratio = penalty / scale
            primal = 0.5 * rr + penalty * bn
            dual = ratio * ry - 0.5 * ratio * ratio * rr
            row = jnp.where(at_lane == t, (primal - dual) / (primal + 1.0), row)
            wide = jnp.concatenate([scale] * (width // 128), axis=1)
            for k, block in enumerate((n0, n1, n2, n3)):
                start = block_at(k, width)
                correlations[t : t + 1, pl.ds(start, width)] = block[t : t + 1, :] / wide
        for t in range(ITERS + 1):
            gaps[t] = jnp.sum(jnp.where(at_lane == t, row, 0.0))
        for t in range(ITERS):
            counts[t] = jnp.sum(jnp.where(at_lane == 8 * t + 4, sums, 0.0))

    outs = [shape_of((ITERS + 1, 4 * width)), shape_of((ITERS + 1,)), shape_of((ITERS,))]
    return call(body, outs, everyone, tops, index, *blocks, smem=(2,), smem_outs=(1, 2))


def turned_back(blocks):
    tasks, width = blocks[0].shape

    def body(c0, c1, c2, c3, out):
        for k, block in enumerate((c0, c1, c2, c3)):
            out[pl.ds(block_at(k, width), width), :] = block[...].T

    return call(body, shape_of((4 * width, tasks)), *blocks)


def to_owners(blocks):
    return [blocks[0]] + [shifted(blocks[k], "samp", k) for k in (1, 3, 2)]


def from_owners(value):
    got = {k: shifted(value, "samp", -k) for k in (1, 3, 2)}
    return [value, got[1], got[2], got[3]]


def plane_exchange(blocks):
    return lax.all_to_all(blocks, PLANE, split_axis=0, concat_axis=0, tiled=True)


def local(design, targets, warm_start, active_mask, penalty_index):
    rows, _ = design.shape
    half = rows // 2
    planes = lax.axis_size("y") * lax.axis_size("z")
    block = half // planes
    step = 8 * block
    blocks = tops = stats = None
    norms = []
    for t in range(ITERS + 1):
        if t == 0:
            *corr, design, own_targets = corr_first(design, targets, step, block)
            corr = to_owners(corr)
            (far,) = fit_warm(False, design, warm_start, half, step)
            arrived = shifted(far, "core", 1)
            near, current = fit_warm(True, design, warm_start, half, step)
            sums, steps, top = joined(near, arrived, planes, corr)
            copies, stats = residual_of(plane_exchange(sums), own_targets, 0, top=top)
        else:
            far = fit_rows(False, design, blocks, half, step)
            arrived = shifted(far, "core", 1)
            near = fit_rows(True, design, blocks, half, step)
            (sums,) = joined(near, arrived, planes)
            copies, stats = residual_of(plane_exchange(sums), own_targets, 8 * t, stats)
        near_rows = plane_exchange(copies)
        far_rows = shifted(near_rows, "core", 1)
        grad = grad_near(design, near_rows, block)
        shares = to_owners(
            grad_far(design, far_rows, grad, block, near_rows if t == 0 else None)
        )
        if t < ITERS:
            current, sent, own_norms, stats, tops = prox(
                shares, current, steps, active_mask, penalty_index, stats, 8 * t,
                BF if t + 1 < ITERS else F32, tops,
            )
            norms.append(own_norms)
            blocks = from_owners(sent)
            if t + 1 == ITERS:
                coefficients = turned_back(blocks)
        else:
            packed = last_norms(shares, current, stats, *norms, 8 * t)
    norm_blocks = from_owners(packed)
    features = planes * lax.axis_size("core")
    copies = of_samples(norm_blocks, features)
    everyone = lax.all_to_all(copies[:, None, :], FEAT, split_axis=0, concat_axis=0, tiled=True)
    correlations, gaps, counts = finish(
        everyone.reshape(copies.shape), tops, penalty_index, norm_blocks
    )
    return coefficients, correlations, gaps, counts


def solution(mesh):
    torus = Mesh(
        mesh.devices.reshape(4, 8, 2, mesh.shape["samp"]), ("y", "z", "core", "samp")
    )
    in_specs = (P("samp", FEAT), P("samp", None), P(FEAT, None), P(None, FEAT), P())
    out_specs = (P(FEAT, None), P(None, FEAT), P(), P())
    return jax.shard_map(
        local, mesh=torus, in_specs=in_specs, out_specs=out_specs, check_vma=False
    )
```

profile of v0, /device:TPU:1, one launch (start us, length us, event | category | flops | bytes accessed | tf_op | source)
XLA Modules:
  0.0 244.6 jit_solution(12961963246463044305)
XLA Ops:
  0.6 5.3 %corr_first.1 = (f32[136,256]{1,0:T(8,128)S(1)}, f32[136,256]{1,0:T(8,128)S(1)}, f32[136,256]{1,0:T(8,128)S(1)}, f32[136,256]{1,0:T(8,128)S(1)}, bf16[3584,1024]...) custom-call(bf16[3584,1024]{1,0:T(8,128)(2,1)} %design.1, bf16[3584,128]{1,0:T(8,128)(2,1)} %targets.1), custom_call_target="tpu_custom_call" | custom-call | tf_op jit(solution)/shard_map/corr_first/pallas_call | solution.py:113
  7.6 3.2 %collective-permute-start = (f32[1792,128]{1,0:T(8,128)S(1)}, f32[1792,128]{1,0:T(8,128)S(1)}, u32[]{:S(2)}, u32[]{:S(2)}) collective-permute-start(f32[1792,128]{1,0:T(8,128)S(1)} %shard_map.85), channel_id=1, source_target_pairs={{0,4},{4,0},{1,5},{5,1},{2,6},{6,2},{3,7},{7,3},{8,12},{12,8},{9,1... | collective-permute-start | bytes 2752520 | tf_op jit(solution)/shard_map/ppermute | solution.py:40
  10.8 2.7 %collective-permute-start.2 = (f32[136,256]{1,0:T(8,128)S(1)}, f32[136,256]{1,0:T(8,128)S(1)}, u32[]{:S(2)}, u32[]{:S(2)}) collective-permute-start(f32[136,256]{1,0:T(8,128)S(1)} %get-tuple-element.50), channel_id=1, source_target_pairs={{0,3},{1,0},{2,1},{3,2},{4,7},{5,4},{6,5},{7,6},{8,11},{9,8},{10,9... | collective-permute-start | bytes 417800 | tf_op jit(solution)/shard_map/ppermute | solution.py:40
  13.5 1.7 shard_map.84
  15.2 1.9 collective-permute-done.1.refs_1_
  17.1 1.8 collective-permute-done.2.refs_2_
  19.9 23.7 %all_to_all.35.parts = bf16[32,56,128]{2,1,0:T(8,128)(2,1)S(1)} all-to-all(bf16[32,56,128]{2,1,0:T(8,128)(2,1)S(1)} %get-tuple-element.52), channel_id=1, replica_groups=mesh['y'=4,'z'=8,'core'=2,'samp'=4] {'y','z'}, dimensions={0} | all-to-all | bytes 917504 | tf_op jit(solution)/shard_map/all_to_all | solution.py:410
  43.8 20.9 %all_to_all.36.right.refs_0_ = bf16[32,64,128]{2,1,0:T(8,128)(2,1)S(1)} all-to-all(bf16[32,64,128]{2,1,0:T(8,128)(2,1)S(1)} %get-tuple-element.55), channel_id=1, replica_groups=mesh['y'=4,'z'=8,'core'=2,'samp'=4] {'y','z'}, dimensions={0} | all-to-all | bytes 1048576 | tf_op jit(solution)/shard_map/all_to_all | solution.py:410
  64.7 4.6 %collective-permute-start.4 = (bf16[32,64,128]{2,1,0:T(8,128)(2,1)S(1)}, bf16[32,64,128]{2,1,0:T(8,128)(2,1)S(1)}, u32[]{:S(2)}, u32[]{:S(2)}) collective-permute-start(bf16[32,64,128]{2,1,0:T(8,128)(2,1)S(1)} %all_to_all.36.right.refs_0_), channel_id=1, source_target_pairs={{0,4},{4,0},{1,5},{5,1},{2,6},{6,2},{3,7},{7,3},{8,12},{12,8},{9,1... | collective-permute-start | bytes 1572872 | tf_op jit(solution)/shard_map/ppermute | solution.py:40
  73.0 2.1 collective-permute-start.6
  75.8 2.7 %collective-permute-done.5.r1 = f32[136,256]{1,0:T(8,128)S(1)} collective-permute-done((f32[136,256]{1,0:T(8,128)S(1)}, f32[136,256]{1,0:T(8,128)S(1)}, u32[]{:S(2)}, u32[]{:S(2)}) %collective-permute-start.5) | collective-permute-done | bytes 139296 | tf_op jit(solution)/shard_map/ppermute | solution.py:40
  78.5 2.4 collective-permute-done.7.r3
  82.3 2.1 collective-permute-start.9
  89.5 4.0 %collective-permute-start.11 = (f32[1792,128]{1,0:T(8,128)S(1)}, f32[1792,128]{1,0:T(8,128)S(1)}, u32[]{:S(2)}, u32[]{:S(2)}) collective-permute-start(f32[1792,128]{1,0:T(8,128)S(1)} %shard_map.92), channel_id=1, source_target_pairs={{0,4},{4,0},{1,5},{5,1},{2,6},{6,2},{3,7},{7,3},{8,12},{12,8},{9,1... | collective-permute-start | bytes 2752520 | tf_op jit(solution)/shard_map/ppermute | solution.py:40
  95.6 17.9 %all_to_all.37.parts = bf16[32,56,128]{2,1,0:T(8,128)(2,1)S(1)} all-to-all(bf16[32,56,128]{2,1,0:T(8,128)(2,1)S(1)} %shard_map.93), channel_id=1, replica_groups=mesh['y'=4,'z'=8,'core'=2,'samp'=4] {'y','z'}, dimensions={0} | all-to-all | bytes 917504 | tf_op jit(solution)/shard_map/all_to_all | solution.py:410
  113.7 19.7 %all_to_all.38.right = bf16[32,56,128]{2,1,0:T(8,128)(2,1)S(1)} all-to-all(bf16[32,56,128]{2,1,0:T(8,128)(2,1)S(1)} %get-tuple-element.65), channel_id=1, replica_groups=mesh['y'=4,'z'=8,'core'=2,'samp'=4] {'y','z'}, dimensions={0} | all-to-all | bytes 917504 | tf_op jit(solution)/shard_map/all_to_all | solution.py:410
  133.5 4.1 %collective-permute-start.12 = (bf16[32,56,128]{2,1,0:T(8,128)(2,1)S(1)}, bf16[32,56,128]{2,1,0:T(8,128)(2,1)S(1)}, u32[]{:S(2)}, u32[]{:S(2)}) collective-permute-start(bf16[32,56,128]{2,1,0:T(8,128)(2,1)S(1)} %all_to_all.38.right), channel_id=1, source_target_pairs={{0,4},{4,0},{1,5},{5,1},{2,6},{6,2},{3,7},{7,3},{8,12},{12,8},{9,1... | collective-permute-start | bytes 1376264 | tf_op jit(solution)/shard_map/ppermute | solution.py:40
  140.6 2.7 %collective-permute-start.14 = (f32[128,256]{1,0:T(8,128)S(1)}, f32[128,256]{1,0:T(8,128)S(1)}, u32[]{:S(2)}, u32[]{:S(2)}) collective-permute-start(f32[128,256]{1,0:T(8,128)S(1)} %get-tuple-element.68), channel_id=1, source_target_pairs={{0,3},{1,0},{2,1},{3,2},{4,7},{5,4},{6,5},{7,6},{8,11},{9,8},{10,9... | collective-permute-start | bytes 393224 | tf_op jit(solution)/shard_map/ppermute | solution.py:40
  143.2 3.2 %collective-permute-done.13.r1 = f32[128,256]{1,0:T(8,128)S(1)} collective-permute-done((f32[128,256]{1,0:T(8,128)S(1)}, f32[128,256]{1,0:T(8,128)S(1)}, u32[]{:S(2)}, u32[]{:S(2)}) %collective-permute-start.13) | collective-permute-done | bytes 131104 | tf_op jit(solution)/shard_map/ppermute | solution.py:40
  146.4 1.9 collective-permute-done.14.r2
  150.1 3.3 %collective-permute-start.17 = (f32[128,256]{1,0:T(8,128)S(1)}, f32[128,256]{1,0:T(8,128)S(1)}, u32[]{:S(2)}, u32[]{:S(2)}) collective-permute-start(f32[128,256]{1,0:T(8,128)S(1)} %get-tuple-element.73.c0), channel_id=1, source_target_pairs={{0,2},{1,3},{2,0},{3,1},{4,6},{5,7},{6,4},{7,5},{8,10},{9,11},{10,... | collective-permute-start | bytes 393224 | tf_op jit(solution)/shard_map/ppermute | solution.py:40
  154.5 3.7 %collective-permute-done.17.c2 = f32[128,256]{1,0:T(8,128)S(1)} collective-permute-done((f32[128,256]{1,0:T(8,128)S(1)}, f32[128,256]{1,0:T(8,128)S(1)}, u32[]{:S(2)}, u32[]{:S(2)}) %collective-permute-start.17) | collective-permute-done | bytes 131104 | tf_op jit(solution)/shard_map/ppermute | solution.py:40
  160.2 2.2 collective-permute-start.19
  164.6 18.2 %all_to_all.39.parts = bf16[32,56,128]{2,1,0:T(8,128)(2,1)S(1)} all-to-all(bf16[32,56,128]{2,1,0:T(8,128)(2,1)S(1)} %shard_map.101), channel_id=1, replica_groups=mesh['y'=4,'z'=8,'core'=2,'samp'=4] {'y','z'}, dimensions={0} | all-to-all | bytes 917504 | tf_op jit(solution)/shard_map/all_to_all | solution.py:410
  183.0 19.7 %all_to_all.40.right = bf16[32,56,128]{2,1,0:T(8,128)(2,1)S(1)} all-to-all(bf16[32,56,128]{2,1,0:T(8,128)(2,1)S(1)} %get-tuple-element.75), channel_id=1, replica_groups=mesh['y'=4,'z'=8,'core'=2,'samp'=4] {'y','z'}, dimensions={0} | all-to-all | bytes 917504 | tf_op jit(solution)/shard_map/all_to_all | solution.py:410
  202.7 4.1 %collective-permute-start.20 = (bf16[32,56,128]{2,1,0:T(8,128)(2,1)S(1)}, bf16[32,56,128]{2,1,0:T(8,128)(2,1)S(1)}, u32[]{:S(2)}, u32[]{:S(2)}) collective-permute-start(bf16[32,56,128]{2,1,0:T(8,128)(2,1)S(1)} %all_to_all.40.right), channel_id=1, source_target_pairs={{0,4},{4,0},{1,5},{5,1},{2,6},{6,2},{3,7},{7,3},{8,12},{12,8},{9,1... | collective-permute-start | bytes 1376264 | tf_op jit(solution)/shard_map/ppermute | solution.py:40
  209.8 2.7 %collective-permute-start.22 = (f32[128,256]{1,0:T(8,128)S(1)}, f32[128,256]{1,0:T(8,128)S(1)}, u32[]{:S(2)}, u32[]{:S(2)}) collective-permute-start(f32[128,256]{1,0:T(8,128)S(1)} %get-tuple-element.78), channel_id=1, source_target_pairs={{0,3},{1,0},{2,1},{3,2},{4,7},{5,4},{6,5},{7,6},{8,11},{9,8},{10,9... | collective-permute-start | bytes 393224 | tf_op jit(solution)/shard_map/ppermute | solution.py:40
  212.8 2.9 %collective-permute-done.21.r1 = f32[128,256]{1,0:T(8,128)S(1)} collective-permute-done((f32[128,256]{1,0:T(8,128)S(1)}, f32[128,256]{1,0:T(8,128)S(1)}, u32[]{:S(2)}, u32[]{:S(2)}) %collective-permute-start.21) | collective-permute-done | bytes 131104 | tf_op jit(solution)/shard_map/ppermute | solution.py:40
  215.7 2.7 %collective-permute-done.23.r3 = f32[128,256]{1,0:T(8,128)S(1)} collective-permute-done((f32[128,256]{1,0:T(8,128)S(1)}, f32[128,256]{1,0:T(8,128)S(1)}, u32[]{:S(2)}, u32[]{:S(2)}) %collective-permute-start.23) | collective-permute-done | bytes 131104 | tf_op jit(solution)/shard_map/ppermute | solution.py:40
  219.6 2.8 %collective-permute-start.25 = (f32[8,256]{1,0:T(8,128)S(1)}, f32[8,256]{1,0:T(8,128)S(1)}, u32[]{:S(2)}, u32[]{:S(2)}) collective-permute-start(f32[8,256]{1,0:T(8,128)S(1)} %shard_map.105.own.n0), channel_id=1, source_target_pairs={{0,2},{1,3},{2,0},{3,1},{4,6},{5,7},{6,4},{7,5},{8,10},{9,11},{10,... | collective-permute-start | bytes 24584 | tf_op jit(solution)/shard_map/ppermute | solution.py:40
  225.8 8.5 %all-to-all-start.6 = ((f32[64,1,128]{2,1,0:T(1,128)}), f32[64,1,128]{2,1,0:T(1,128)S(1)}, u32[]{:S(2)}, u32[]{:S(2)}) async-start(f32[64,1,128]{2,1,0:T(1,128)} %bitcast.1), calls=%async_computation.6 | async-start | bytes 65536 | tf_op jit(solution)/shard_map/all_to_all | solution.py:456
  235.3 8.3 %all-to-all-done.6 = f32[64,1,128]{2,1,0:T(1,128)S(1)} async-done(((f32[64,1,128]{2,1,0:T(1,128)}), f32[64,1,128]{2,1,0:T(1,128)S(1)}, u32[]{:S(2)}, u32[]{:S(2)}) %all-to-all-start.6) | async-done | bytes 32800 | tf_op jit(solution)/shard_map/all_to_all | solution.py:456
  (59 shorter events, 35.2 us)
Async XLA Ops:
  0.6 5.3 %copy-start = (f32[1024,128]{1,0:T(8,128)S(1)}, f32[1024,128]{1,0:T(8,128)}, u32[]{:S(2)}) copy-start(f32[1024,128]{1,0:T(8,128)} %warm.3) | copy-start | bytes 1572868
  7.6 12.0 %collective-permute-start = (f32[1792,128]{1,0:T(8,128)S(1)}, f32[1792,128]{1,0:T(8,128)S(1)}, u32[]{:S(2)}, u32[]{:S(2)}) collective-permute-start(f32[1792,128]{1,0:T(8,128)S(1)} %shard_map.85), channel_id=1, source_target_pairs={{0,4},{4,0},{1,5},{5,1},{2,6},{6,2},{3,7},{7,3},{8,12},{12,8},{9,1... | collective-permute-start | bytes 2752520 | tf_op jit(solution)/shard_map/ppermute | solution.py:40
  10.8 6.3 %collective-permute-start.1 = (f32[136,256]{1,0:T(8,128)S(1)}, f32[136,256]{1,0:T(8,128)S(1)}, u32[]{:S(2)}, u32[]{:S(2)}) collective-permute-start(f32[136,256]{1,0:T(8,128)S(1)} %get-tuple-element.49), channel_id=1, source_target_pairs={{0,1},{1,2},{2,3},{3,0},{4,5},{5,6},{6,7},{7,4},{8,9},{9,10},{10,1... | collective-permute-start | bytes 417800 | tf_op jit(solution)/shard_map/ppermute | solution.py:40
  10.8 8.2 %collective-permute-start.2 = (f32[136,256]{1,0:T(8,128)S(1)}, f32[136,256]{1,0:T(8,128)S(1)}, u32[]{:S(2)}, u32[]{:S(2)}) collective-permute-start(f32[136,256]{1,0:T(8,128)S(1)} %get-tuple-element.50), channel_id=1, source_target_pairs={{0,3},{1,0},{2,1},{3,2},{4,7},{5,4},{6,5},{7,6},{8,11},{9,8},{10,9... | collective-permute-start | bytes 417800 | tf_op jit(solution)/shard_map/ppermute | solution.py:40
  13.5 6.1 %collective-permute-start.3 = (f32[136,256]{1,0:T(8,128)S(1)}, f32[136,256]{1,0:T(8,128)S(1)}, u32[]{:S(2)}, u32[]{:S(2)}) collective-permute-start(f32[136,256]{1,0:T(8,128)S(1)} %get-tuple-element.51), channel_id=1, source_target_pairs={{0,2},{1,3},{2,0},{3,1},{4,6},{5,7},{6,4},{7,5},{8,10},{9,11},{10,... | collective-permute-start | bytes 417800 | tf_op jit(solution)/shard_map/ppermute | solution.py:40
  64.7 16.3 %copy-start.1 = (s32[2,1024]{1,0:T(2,128)S(1)}, s32[2,1024]{1,0:T(2,128)}, u32[]{:S(2)}) copy-start(s32[2,1024]{1,0:T(2,128)} %mask.3) | copy-start | bytes 24580
  64.7 6.1 %collective-permute-start.4 = (bf16[32,64,128]{2,1,0:T(8,128)(2,1)S(1)}, bf16[32,64,128]{2,1,0:T(8,128)(2,1)S(1)}, u32[]{:S(2)}, u32[]{:S(2)}) collective-permute-start(bf16[32,64,128]{2,1,0:T(8,128)(2,1)S(1)} %all_to_all.36.right.refs_0_), channel_id=1, source_target_pairs={{0,4},{4,0},{1,5},{5,1},{2,6},{6,2},{3,7},{7,3},{8,12},{12,8},{9,1... | collective-permute-start | bytes 1572872 | tf_op jit(solution)/shard_map/ppermute | solution.py:40
  72.4 6.1 %collective-permute-start.5 = (f32[136,256]{1,0:T(8,128)S(1)}, f32[136,256]{1,0:T(8,128)S(1)}, u32[]{:S(2)}, u32[]{:S(2)}) collective-permute-start(f32[136,256]{1,0:T(8,128)S(1)} %get-tuple-element.57), channel_id=1, source_target_pairs={{0,1},{1,2},{2,3},{3,0},{4,5},{5,6},{6,7},{7,4},{8,9},{9,10},{10,1... | collective-permute-start | bytes 417800 | tf_op jit(solution)/shard_map/ppermute | solution.py:40
  73.0 5.5 %collective-permute-start.6 = (f32[136,256]{1,0:T(8,128)S(1)}, f32[136,256]{1,0:T(8,128)S(1)}, u32[]{:S(2)}, u32[]{:S(2)}) collective-permute-start(f32[136,256]{1,0:T(8,128)S(1)} %get-tuple-element.58), channel_id=1, source_target_pairs={{0,3},{1,0},{2,1},{3,2},{4,7},{5,4},{6,5},{7,6},{8,11},{9,8},{10,9... | collective-permute-start | bytes 417800 | tf_op jit(solution)/shard_map/ppermute | solution.py:40
  75.1 5.8 %collective-permute-start.7 = (f32[136,256]{1,0:T(8,128)S(1)}, f32[136,256]{1,0:T(8,128)S(1)}, u32[]{:S(2)}, u32[]{:S(2)}) collective-permute-start(f32[136,256]{1,0:T(8,128)S(1)} %get-tuple-element.59), channel_id=1, source_target_pairs={{0,2},{1,3},{2,0},{3,1},{4,6},{5,7},{6,4},{7,5},{8,10},{9,11},{10,... | collective-permute-start | bytes 417800 | tf_op jit(solution)/shard_map/ppermute | solution.py:40
  81.1 4.4 %collective-permute-start.10 = (bf16[128,256]{1,0:T(8,128)(2,1)S(1)}, bf16[128,256]{1,0:T(8,128)(2,1)S(1)}, u32[]{:S(2)}, u32[]{:S(2)}) collective-permute-start(bf16[128,256]{1,0:T(8,128)(2,1)S(1)} %get-tuple-element.63.c0), channel_id=1, source_target_pairs={{0,1},{1,2},{2,3},{3,0},{4,5},{5,6},{6,7},{7,4},{8,9},{9,10},{10,1... | collective-permute-start | bytes 196616 | tf_op jit(solution)/shard_map/ppermute | solution.py:40
  82.3 4.6 %collective-permute-start.9 = (bf16[128,256]{1,0:T(8,128)(2,1)S(1)}, bf16[128,256]{1,0:T(8,128)(2,1)S(1)}, u32[]{:S(2)}, u32[]{:S(2)}) collective-permute-start(bf16[128,256]{1,0:T(8,128)(2,1)S(1)} %get-tuple-element.63.c0), channel_id=1, source_target_pairs={{0,2},{1,3},{2,0},{3,1},{4,6},{5,7},{6,4},{7,5},{8,10},{9,11},{10,... | collective-permute-start | bytes 196616 | tf_op jit(solution)/shard_map/ppermute | solution.py:40
  84.4 3.4 %collective-permute-start.8 = (bf16[128,256]{1,0:T(8,128)(2,1)S(1)}, bf16[128,256]{1,0:T(8,128)(2,1)S(1)}, u32[]{:S(2)}, u32[]{:S(2)}) collective-permute-start(bf16[128,256]{1,0:T(8,128)(2,1)S(1)} %get-tuple-element.63.c0), channel_id=1, source_target_pairs={{0,3},{1,0},{2,1},{3,2},{4,7},{5,4},{6,5},{7,6},{8,11},{9,8},{10,9... | collective-permute-start | bytes 196616 | tf_op jit(solution)/shard_map/ppermute | solution.py:40
  89.5 6.1 %collective-permute-start.11 = (f32[1792,128]{1,0:T(8,128)S(1)}, f32[1792,128]{1,0:T(8,128)S(1)}, u32[]{:S(2)}, u32[]{:S(2)}) collective-permute-start(f32[1792,128]{1,0:T(8,128)S(1)} %shard_map.92), channel_id=1, source_target_pairs={{0,4},{4,0},{1,5},{5,1},{2,6},{6,2},{3,7},{7,3},{8,12},{12,8},{9,1... | collective-permute-start | bytes 2752520 | tf_op jit(solution)/shard_map/ppermute | solution.py:40
  133.5 5.6 %collective-permute-start.12 = (bf16[32,56,128]{2,1,0:T(8,128)(2,1)S(1)}, bf16[32,56,128]{2,1,0:T(8,128)(2,1)S(1)}, u32[]{:S(2)}, u32[]{:S(2)}) collective-permute-start(bf16[32,56,128]{2,1,0:T(8,128)(2,1)S(1)} %all_to_all.38.right), channel_id=1, source_target_pairs={{0,4},{4,0},{1,5},{5,1},{2,6},{6,2},{3,7},{7,3},{8,12},{12,8},{9,1... | collective-permute-start | bytes 1376264 | tf_op jit(solution)/shard_map/ppermute | solution.py:40
  140.5 6.0 %collective-permute-start.13 = (f32[128,256]{1,0:T(8,128)S(1)}, f32[128,256]{1,0:T(8,128)S(1)}, u32[]{:S(2)}, u32[]{:S(2)}) collective-permute-start(f32[128,256]{1,0:T(8,128)S(1)} %get-tuple-element.67), channel_id=1, source_target_pairs={{0,1},{1,2},{2,3},{3,0},{4,5},{5,6},{6,7},{7,4},{8,9},{9,10},{10,1... | collective-permute-start | bytes 393224 | tf_op jit(solution)/shard_map/ppermute | solution.py:40
  140.6 7.8 %collective-permute-start.14 = (f32[128,256]{1,0:T(8,128)S(1)}, f32[128,256]{1,0:T(8,128)S(1)}, u32[]{:S(2)}, u32[]{:S(2)}) collective-permute-start(f32[128,256]{1,0:T(8,128)S(1)} %get-tuple-element.68), channel_id=1, source_target_pairs={{0,3},{1,0},{2,1},{3,2},{4,7},{5,4},{6,5},{7,6},{8,11},{9,8},{10,9... | collective-permute-start | bytes 393224 | tf_op jit(solution)/shard_map/ppermute | solution.py:40
  143.2 5.6 %collective-permute-start.15 = (f32[128,256]{1,0:T(8,128)S(1)}, f32[128,256]{1,0:T(8,128)S(1)}, u32[]{:S(2)}, u32[]{:S(2)}) collective-permute-start(f32[128,256]{1,0:T(8,128)S(1)} %get-tuple-element.69), channel_id=1, source_target_pairs={{0,2},{1,3},{2,0},{3,1},{4,6},{5,7},{6,4},{7,5},{8,10},{9,11},{10,... | collective-permute-start | bytes 393224 | tf_op jit(solution)/shard_map/ppermute | solution.py:40
  149.0 5.5 %collective-permute-start.18 = (f32[128,256]{1,0:T(8,128)S(1)}, f32[128,256]{1,0:T(8,128)S(1)}, u32[]{:S(2)}, u32[]{:S(2)}) collective-permute-start(f32[128,256]{1,0:T(8,128)S(1)} %get-tuple-element.73.c0), channel_id=1, source_target_pairs={{0,1},{1,2},{2,3},{3,0},{4,5},{5,6},{6,7},{7,4},{8,9},{9,10},{10,1... | collective-permute-start | bytes 393224 | tf_op jit(solution)/shard_map/ppermute | solution.py:40
  150.1 8.1 %collective-permute-start.17 = (f32[128,256]{1,0:T(8,128)S(1)}, f32[128,256]{1,0:T(8,128)S(1)}, u32[]{:S(2)}, u32[]{:S(2)}) collective-permute-start(f32[128,256]{1,0:T(8,128)S(1)} %get-tuple-element.73.c0), channel_id=1, source_target_pairs={{0,2},{1,3},{2,0},{3,1},{4,6},{5,7},{6,4},{7,5},{8,10},{9,11},{10,... | collective-permute-start | bytes 393224 | tf_op jit(solution)/shard_map/ppermute | solution.py:40
  153.4 5.2 %collective-permute-start.16 = (f32[128,256]{1,0:T(8,128)S(1)}, f32[128,256]{1,0:T(8,128)S(1)}, u32[]{:S(2)}, u32[]{:S(2)}) collective-permute-start(f32[128,256]{1,0:T(8,128)S(1)} %get-tuple-element.73.c0), channel_id=1, source_target_pairs={{0,3},{1,0},{2,1},{3,2},{4,7},{5,4},{6,5},{7,6},{8,11},{9,8},{10,9... | collective-permute-start | bytes 393224 | tf_op jit(solution)/shard_map/ppermute | solution.py:40
  160.2 4.3 %collective-permute-start.19 = (f32[1792,128]{1,0:T(8,128)S(1)}, f32[1792,128]{1,0:T(8,128)S(1)}, u32[]{:S(2)}, u32[]{:S(2)}) collective-permute-start(f32[1792,128]{1,0:T(8,128)S(1)} %shard_map.100), channel_id=1, source_target_pairs={{0,4},{4,0},{1,5},{5,1},{2,6},{6,2},{3,7},{7,3},{8,12},{12,8},{9,1... | collective-permute-start | bytes 2752520 | tf_op jit(solution)/shard_map/ppermute | solution.py:40
  202.7 5.6 %collective-permute-start.20 = (bf16[32,56,128]{2,1,0:T(8,128)(2,1)S(1)}, bf16[32,56,128]{2,1,0:T(8,128)(2,1)S(1)}, u32[]{:S(2)}, u32[]{:S(2)}) collective-permute-start(bf16[32,56,128]{2,1,0:T(8,128)(2,1)S(1)} %all_to_all.40.right), channel_id=1, source_target_pairs={{0,4},{4,0},{1,5},{5,1},{2,6},{6,2},{3,7},{7,3},{8,12},{12,8},{9,1... | collective-permute-start | bytes 1376264 | tf_op jit(solution)/shard_map/ppermute | solution.py:40
  209.7 6.0 %collective-permute-start.21 = (f32[128,256]{1,0:T(8,128)S(1)}, f32[128,256]{1,0:T(8,128)S(1)}, u32[]{:S(2)}, u32[]{:S(2)}) collective-permute-start(f32[128,256]{1,0:T(8,128)S(1)} %get-tuple-element.77), channel_id=1, source_target_pairs={{0,1},{1,2},{2,3},{3,0},{4,5},{5,6},{6,7},{7,4},{8,9},{9,10},{10,1... | collective-permute-start | bytes 393224 | tf_op jit(solution)/shard_map/ppermute | solution.py:40
  209.8 5.9 %collective-permute-start.22 = (f32[128,256]{1,0:T(8,128)S(1)}, f32[128,256]{1,0:T(8,128)S(1)}, u32[]{:S(2)}, u32[]{:S(2)}) collective-permute-start(f32[128,256]{1,0:T(8,128)S(1)} %get-tuple-element.78), channel_id=1, source_target_pairs={{0,3},{1,0},{2,1},{3,2},{4,7},{5,4},{6,5},{7,6},{8,11},{9,8},{10,9... | collective-permute-start | bytes 393224 | tf_op jit(solution)/shard_map/ppermute | solution.py:40
  212.5 5.9 %collective-permute-start.23 = (f32[128,256]{1,0:T(8,128)S(1)}, f32[128,256]{1,0:T(8,128)S(1)}, u32[]{:S(2)}, u32[]{:S(2)}) collective-permute-start(f32[128,256]{1,0:T(8,128)S(1)} %get-tuple-element.79), channel_id=1, source_target_pairs={{0,2},{1,3},{2,0},{3,1},{4,6},{5,7},{6,4},{7,5},{8,10},{9,11},{10,... | collective-permute-start | bytes 393224 | tf_op jit(solution)/shard_map/ppermute | solution.py:40
  218.6 3.8 %collective-permute-start.26 = (f32[8,256]{1,0:T(8,128)S(1)}, f32[8,256]{1,0:T(8,128)S(1)}, u32[]{:S(2)}, u32[]{:S(2)}) collective-permute-start(f32[8,256]{1,0:T(8,128)S(1)} %shard_map.105.own.n0), channel_id=1, source_target_pairs={{0,1},{1,2},{2,3},{3,0},{4,5},{5,6},{6,7},{7,4},{8,9},{9,10},{10,1... | collective-permute-start | bytes 24584 | tf_op jit(solution)/shard_map/ppermute | solution.py:40
  219.6 4.0 %collective-permute-start.25 = (f32[8,256]{1,0:T(8,128)S(1)}, f32[8,256]{1,0:T(8,128)S(1)}, u32[]{:S(2)}, u32[]{:S(2)}) collective-permute-start(f32[8,256]{1,0:T(8,128)S(1)} %shard_map.105.own.n0), channel_id=1, source_target_pairs={{0,2},{1,3},{2,0},{3,1},{4,6},{5,7},{6,4},{7,5},{8,10},{9,11},{10,... | collective-permute-start | bytes 24584 | tf_op jit(solution)/shard_map/ppermute | solution.py:40
  222.4 2.8 %collective-permute-start.24 = (f32[8,256]{1,0:T(8,128)S(1)}, f32[8,256]{1,0:T(8,128)S(1)}, u32[]{:S(2)}, u32[]{:S(2)}) collective-permute-start(f32[8,256]{1,0:T(8,128)S(1)} %shard_map.105.own.n0), channel_id=1, source_target_pairs={{0,3},{1,0},{2,1},{3,2},{4,7},{5,4},{6,5},{7,6},{8,11},{9,8},{10,9... | collective-permute-start | bytes 24584 | tf_op jit(solution)/shard_map/ppermute | solution.py:40
  225.8 17.8 %all-to-all-start.6 = ((f32[64,1,128]{2,1,0:T(1,128)}), f32[64,1,128]{2,1,0:T(1,128)S(1)}, u32[]{:S(2)}, u32[]{:S(2)}) async-start(f32[64,1,128]{2,1,0:T(1,128)} %bitcast.1), calls=%async_computation.6 | async-start | bytes 65536 | tf_op jit(solution)/shard_map/all_to_all | solution.py:456
where the time goes:
time: 245 us
  blocking collectives  120 us (49%)
  starting transfers between devices  54 us (22%)
  waiting for transfers between devices  41.2 us (17%)
  Pallas kernels  27.6 us (11%)
    all_to_all x6, blocking collectives, plane_exchange(): lax.all_to_all(blocks, PLANE, split_axis=0, concat_axis=0, tiled=True)  120 us
    ppermute x27, starting transfers between devices, shifted(): return lax.ppermute(value, axis, [(i, (i + by) % n) for i in range(n)])  45.5 us
    ppermute x27, waiting for transfers between devices, shifted(): return lax.ppermute(value, axis, [(i, (i + by) % n) for i in range(n)])  32.9 us
    pallas_call x24, Pallas kernels, call(): pl.pallas_call(body, out_shape=shapes[0] if single else tuple(shapes), in...  22.4 us
    all_to_all x1, starting transfers between devices, local(): lax.all_to_all(copies[:, None, :], FEAT, split_axis=0, concat_axis=0, til...  8.49 us
    all_to_all x1, waiting for transfers between devices, local(): lax.all_to_all(copies[:, None, :], FEAT, split_axis=0, concat_axis=0, til...  8.31 us
    pallas_call x1, Pallas kernels, corr_first(): pl.pallas_call(body, out_shape=(*[shape_of((tasks + 8, width))] * 4, pltp...  5.25 us
  transfers between devices with their start and end apart: 28, of which 24 were waited for; matrix products, arithmetic and copies ran while one was open for 0% of the time, Pallas kernels for 4%

commit v1 on v0

--- a/solution.py
+++ b/solution.py
@@ -9,6 +9,7 @@
 
 ITERS = 2
 FEAT = ("y", "z", "core")
+ALL = ("y", "z", "core", "samp")
 PLANE = ("y", "z")
 BF = jnp.bfloat16
 F32 = jnp.float32
@@ -152,7 +153,39 @@
     return call(body, outs, design, warm)
 
 
-def fit_rows(near, design, blocks, rows, step):
+def fit_rows(near, design, blocks, ks, rows, step, start=None):
+    tasks, width = blocks[0].shape
+    given = [] if start is None else [start]
+
+    def body(design, *refs):
+        *blocks, out, whole = refs
+        for k, block in zip(range(len(ks)), blocks):
+            whole[:, k * width : (k + 1) * width] = block[...].astype(BF)
+
+        def one(i, carry):
+            at = pl.multiple_of(half_start(near, rows) + i * step, step)
+            here = pl.ds(pl.multiple_of(i * step, step), step)
+            total = blocks[-1][here, :] if given else None
+            for n, k in enumerate(ks):
+                part = lax.dot_general(
+                    design[pl.ds(at, step), pl.ds(block_at(k, width), width)],
+                    whole[:, n * width : (n + 1) * width],
+                    (((1,), (1,)), ((), ())),
+                    preferred_element_type=F32,
+                )
+                total = part if total is None else total + part
+            out[here, :] = total
+            return carry
+
+        lax.fori_loop(0, rows // step, one, 0)
+
+    return call(
+        body, shape_of((rows, tasks)), design, *[blocks[k] for k in ks], *given,
+        scratch=[pltpu.VMEM((tasks, len(ks) * width), BF)],
+    )
+
+
+def fit_all(design, blocks, rows, step):
     tasks, width = blocks[0].shape
 
     def body(design, c0, c1, c2, c3, out, whole):
@@ -160,7 +193,7 @@
             whole[:, pl.ds(block_at(k, width), width)] = block[...].astype(BF)
 
         def one(i, carry):
-            at = pl.multiple_of(half_start(near, rows) + i * step, step)
+            at = pl.multiple_of(half_start(True, rows) + i * step, step)
             out[pl.ds(pl.multiple_of(i * step, step), step), :] = lax.dot_general(
                 design[pl.ds(at, step), :],
                 whole[...],
@@ -230,26 +263,38 @@
     return jnp.max(jnp.sum(pieces, axis=1))
 
 
-def grad_far(design, right, start, block, near=None):
+def grad_far(ks, design, right, start, block, near=None):
     tasks, cols = start.shape
     width = cols // 4
     extra = 0 if near is None else EXTRA
+    planes = right.shape[0]
+    group = 8
+    step = group * block
 
     def body(design, right, start, *refs):
-        outs, total = refs[-5:-1], refs[-1]
-        total[...] = start[...]
-        grad_loop(False, right, design, total, block)
-        for k, out in enumerate(outs):
-            at = block_at(k, width)
-            out[:tasks, :] = total[:, pl.ds(at, width)]
+        outs = refs[-len(ks) :]
+        for k, out in zip(ks, outs):
+            out[:tasks, :] = start[:, pl.ds(block_at(k, width), width)]
+
+        def one(i, carry):
+            rows = right[pl.ds(i * group, group)].astype(F32)[:, :block]
+            rows = rows.reshape(step, tasks).astype(BF)
+            at = pl.multiple_of(half_start(False, planes * block) + i * step, step)
+            for k, out in zip(ks, outs):
+                out[:tasks, :] += turned_dot(
+                    rows, design[pl.ds(at, step), pl.ds(block_at(k, width), width)]
+                )
+            return carry
+
+        lax.fori_loop(0, planes // group, one, 0)
         if extra:
             top = jnp.maximum(top_of(right, block), top_of(refs[0], block))
             for out in outs:
                 out[tasks:, :] = jnp.full((extra, width), top, F32)
 
-    outs = [shape_of((tasks + extra, width))] * 4
+    outs = [shape_of((tasks + extra, width))] * len(ks)
     args = [design, right, start] + ([] if near is None else [near])
-    return call(body, outs, *args, scratch=[pltpu.VMEM((tasks, cols), F32)])
+    return call(body, outs, *args)
 
 
 def residual_of(parts, own, at, stats=None, top=None):
@@ -327,28 +372,16 @@
     return call(body, outs, *args, smem=(7,))
 
 
-def last_norms(parts, current, stats, n0, n1, at):
-    width = n0.shape[1]
-
-    def body(own, r1, r2, r3, current, stats, n0, n1, out):
+def last_norms(parts, current, stats, n0, n1, at, devices):
+    def body(own, r1, r2, r3, current, stats, n0, n1, norms_out, copies):
         norms = lane_norms(own[...] + r1[...] + r2[...] + r3[...])
+        norms_out[...] = jnp.concatenate([n0[...], n1[...], norms] + [norms] * 5, axis=0)
         row = lane(stats[...], at + 2, jnp.sum(lane_norms(current[...])))
         row = lane(row, at + 3, jnp.max(norms))
-        wide = jnp.concatenate([row] * (width // row.shape[1]), axis=1)
-        out[...] = jnp.concatenate([n0[...], n1[...], norms] + [wide] * 5, axis=0)
-
-    return call(body, shape_of((8, width)), *parts, current, stats, n0, n1)
-
-
-def of_samples(blocks, copies):
-    def body(own, n1, n2, n3, out):
-        rows = [ref[3:4, 0:128] for ref in (own, n1, n2, n3)]
-        total = (rows[0] + rows[2]) + (rows[1] + rows[3])
-        high = jnp.maximum(jnp.maximum(rows[0], rows[2]), jnp.maximum(rows[1], rows[3]))
-        at = lax.broadcasted_iota(jnp.int32, total.shape, 1)
-        out[...] = jnp.broadcast_to(jnp.where((at & 7) == 3, high, total), out.shape)
-
-    return call(body, shape_of((copies, 128)), *blocks)
+        copies[...] = jnp.broadcast_to(row, copies.shape)
+
+    outs = [shape_of((8, n0.shape[1])), shape_of((devices, stats.shape[1]))]
+    return call(body, outs, *parts, current, stats, n0, n1)
 
 
 def finish(everyone, tops, index, blocks):
@@ -416,44 +449,60 @@
     planes = lax.axis_size("y") * lax.axis_size("z")
     block = half // planes
     step = 8 * block
-    blocks = tops = stats = None
-    norms = []
-    for t in range(ITERS + 1):
+    devices = 1
+    for axis in ALL:
+        devices *= lax.axis_size(axis)
+
+    state = {"far": None, "blocks": None, "stats": None, "tops": None, "norms": []}
+
+    def iteration(t, design):
         if t == 0:
             *corr, design, own_targets = corr_first(design, targets, step, block)
             corr = to_owners(corr)
             (far,) = fit_warm(False, design, warm_start, half, step)
             arrived = shifted(far, "core", 1)
-            near, current = fit_warm(True, design, warm_start, half, step)
-            sums, steps, top = joined(near, arrived, planes, corr)
+            near, state["current"] = fit_warm(True, design, warm_start, half, step)
+            sums, state["steps"], top = joined(near, arrived, planes, corr)
+            state["own_targets"] = own_targets
             copies, stats = residual_of(plane_exchange(sums), own_targets, 0, top=top)
         else:
-            far = fit_rows(False, design, blocks, half, step)
-            arrived = shifted(far, "core", 1)
-            near = fit_rows(True, design, blocks, half, step)
+            blocks = state["blocks"]
+            arrived = shifted(state["far"], "core", 1)
+            near = fit_all(design, blocks, half, step)
             (sums,) = joined(near, arrived, planes)
-            copies, stats = residual_of(plane_exchange(sums), own_targets, 8 * t, stats)
+            copies, stats = residual_of(
+                plane_exchange(sums), state["own_targets"], 8 * t, state["stats"]
+            )
         near_rows = plane_exchange(copies)
         far_rows = shifted(near_rows, "core", 1)
         grad = grad_near(design, near_rows, block)
-        shares = to_owners(
-            grad_far(design, far_rows, grad, block, near_rows if t == 0 else None)
+        given = near_rows if t == 0 else None
+        b2, b1 = grad_far((2, 1), design, far_rows, grad, block, given)
+        r2, r1 = shifted(b2, "samp", 2), shifted(b1, "samp", 1)
+        b3, b0 = grad_far((3, 0), design, far_rows, grad, block, given)
+        shares = [b0, r1, shifted(b3, "samp", 3), r2]
+        if t == ITERS:
+            return last_norms(shares, state["current"], stats, *state["norms"], 8 * t, devices)
+        state["current"], sent, own_norms, state["stats"], state["tops"] = prox(
+            shares, state["current"], state["steps"], active_mask, penalty_index, stats, 8 * t,
+            BF if t + 1 < ITERS else F32, state["tops"],
         )
-        if t < ITERS:
-            current, sent, own_norms, stats, tops = prox(
-                shares, current, steps, active_mask, penalty_index, stats, 8 * t,
-                BF if t + 1 < ITERS else F32, tops,
-            )
-            norms.append(own_norms)
-            blocks = from_owners(sent)
-            if t + 1 == ITERS:
-                coefficients = turned_back(blocks)
-        else:
-            packed = last_norms(shares, current, stats, *norms, 8 * t)
+        state["norms"].append(own_norms)
+        c1, c3 = shifted(sent, "samp", -1), shifted(sent, "samp", -3)
+        c2 = shifted(sent, "samp", -2)
+        blocks = state["blocks"] = [sent, c1, c2, c3]
+        far = fit_rows(False, design, blocks, (0,), half, step)
+        far = fit_rows(False, design, blocks, (1, 3), half, step, far)
+        state["far"] = fit_rows(False, design, blocks, (2,), half, step, far)
+        return design
+
+    for t in range(ITERS):
+        design = iteration(t, design)
+    coefficients = turned_back(state["blocks"])
+    packed, copies = iteration(ITERS, design)
+    tops = state["tops"]
     norm_blocks = from_owners(packed)
-    features = planes * lax.axis_size("core")
-    copies = of_samples(norm_blocks, features)
-    everyone = lax.all_to_all(copies[:, None, :], FEAT, split_axis=0, concat_axis=0, tiled=True)
+    everyone = lax.all_to_all(copies[:, None, :], ALL, split_axis=0, concat_axis=0, tiled=True)
     correlations, gaps, counts = finish(
         everyone.reshape(copies.shape), tops, penalty_index, norm_blocks
     )

time: 245 us -> 245 us (level)
  waiting for transfers between devices: 41.2 us -> 36.3 us
  Pallas kernels: 27.6 us -> 32.5 us
    pallas_call x24 -> x30, Pallas kernels: 22.4 us -> 27.2 us  [call(): pl.pallas_call(body, out_shape=shapes[0] if single else tuple(shapes), in...]
    all_to_all x1, waiting for transfers between devices: 8.31 us -> 5.49 us  [local(): lax.all_to_all(copies[:, None, :], ALL, split_axis=0, concat_axis=0, tile...]
  transfers between devices with their start and end apart: 28 -> 28, of which waited for: 24 -> 22; matrix products, arithmetic and copies ran while one was open for 0% -> 0% of each run, Pallas kernels for 4% -> 7%
where the time goes in v1:
time: 245 us
  blocking collectives  120 us (49%)
  starting transfers between devices  53.8 us (22%)
  waiting for transfers between devices  36.3 us (15%)
  Pallas kernels  32.5 us (13%)
    all_to_all x6, blocking collectives, plane_exchange(): lax.all_to_all(blocks, PLANE, split_axis=0, concat_axis=0, tiled=True)  120 us
    ppermute x27, starting transfers between devices, shifted(): return lax.ppermute(value, axis, [(i, (i + by) % n) for i in range(n)])  44.5 us
    ppermute x27, waiting for transfers between devices, shifted(): return lax.ppermute(value, axis, [(i, (i + by) % n) for i in range(n)])  30.9 us
    pallas_call x30, Pallas kernels, call(): pl.pallas_call(body, out_shape=shapes[0] if single else tuple(shapes), in...  27.2 us
    all_to_all x1, starting transfers between devices, local(): lax.all_to_all(copies[:, None, :], ALL, split_axis=0, concat_axis=0, tile...  9.32 us
    all_to_all x1, waiting for transfers between devices, local(): lax.all_to_all(copies[:, None, :], ALL, split_axis=0, concat_axis=0, tile...  5.49 us
    pallas_call x1, Pallas kernels, corr_first(): pl.pallas_call(body, out_shape=(*[shape_of((tasks + 8, width))] * 4, pltp...  5.25 us
  transfers between devices with their start and end apart: 28, of which 22 were waited for; matrix products, arithmetic and copies ran while one was open for 0% of the time, Pallas kernels for 7%

profile of v1, /device:TPU:1, one launch (start us, length us, event | category | flops | bytes accessed | tf_op | source)
XLA Modules:
  0.0 244.5 jit_solution(6446199058394160145)
XLA Ops:
  0.6 5.3 %corr_first.1 = (f32[136,256]{1,0:T(8,128)S(1)}, f32[136,256]{1,0:T(8,128)S(1)}, f32[136,256]{1,0:T(8,128)S(1)}, f32[136,256]{1,0:T(8,128)S(1)}, bf16[3584,1024]...) custom-call(bf16[3584,1024]{1,0:T(8,128)(2,1)} %design.1, bf16[3584,128]{1,0:T(8,128)(2,1)} %targets.1), custom_call_target="tpu_custom_call" | custom-call | tf_op jit(solution)/shard_map/corr_first/pallas_call | solution.py:114
  5.9 1.6 shard_map.85
  7.6 3.2 %collective-permute-start = (f32[1792,128]{1,0:T(8,128)S(1)}, f32[1792,128]{1,0:T(8,128)S(1)}, u32[]{:S(2)}, u32[]{:S(2)}) collective-permute-start(f32[1792,128]{1,0:T(8,128)S(1)} %shard_map.85), channel_id=1, source_target_pairs={{0,4},{4,0},{1,5},{5,1},{2,6},{6,2},{3,7},{7,3},{8,12},{12,8},{9,1... | collective-permute-start | bytes 2752520 | tf_op jit(solution)/shard_map/ppermute | solution.py:41
  10.8 2.7 %collective-permute-start.2 = (f32[136,256]{1,0:T(8,128)S(1)}, f32[136,256]{1,0:T(8,128)S(1)}, u32[]{:S(2)}, u32[]{:S(2)}) collective-permute-start(f32[136,256]{1,0:T(8,128)S(1)} %get-tuple-element.52), channel_id=1, source_target_pairs={{0,3},{1,0},{2,1},{3,2},{4,7},{5,4},{6,5},{7,6},{8,11},{9,8},{10,9... | collective-permute-start | bytes 417800 | tf_op jit(solution)/shard_map/ppermute | solution.py:41
  13.5 1.7 shard_map.84
  15.2 1.9 collective-permute-done.1.refs_1_
  17.1 1.8 collective-permute-done.2.refs_2_
  19.9 23.7 %all_to_all.35.parts = bf16[32,56,128]{2,1,0:T(8,128)(2,1)S(1)} all-to-all(bf16[32,56,128]{2,1,0:T(8,128)(2,1)S(1)} %get-tuple-element.54), channel_id=1, replica_groups=mesh['y'=4,'z'=8,'core'=2,'samp'=4] {'y','z'}, dimensions={0} | all-to-all | bytes 917504 | tf_op jit(solution)/shard_map/all_to_all | solution.py:443
  43.8 20.9 %all_to_all.36.right.refs_0_ = bf16[32,64,128]{2,1,0:T(8,128)(2,1)S(1)} all-to-all(bf16[32,64,128]{2,1,0:T(8,128)(2,1)S(1)} %get-tuple-element.57), channel_id=1, replica_groups=mesh['y'=4,'z'=8,'core'=2,'samp'=4] {'y','z'}, dimensions={0} | all-to-all | bytes 1048576 | tf_op jit(solution)/shard_map/all_to_all | solution.py:443
  64.7 4.6 %collective-permute-start.4 = (bf16[32,64,128]{2,1,0:T(8,128)(2,1)S(1)}, bf16[32,64,128]{2,1,0:T(8,128)(2,1)S(1)}, u32[]{:S(2)}, u32[]{:S(2)}) collective-permute-start(bf16[32,64,128]{2,1,0:T(8,128)(2,1)S(1)} %all_to_all.36.right.refs_0_), channel_id=1, source_target_pairs={{0,4},{4,0},{1,5},{5,1},{2,6},{6,2},{3,7},{7,3},{8,12},{12,8},{9,1... | collective-permute-start | bytes 1572872 | tf_op jit(solution)/shard_map/ppermute | solution.py:41
  77.2 1.9 collective-permute-done.5.r1
  82.7 2.3 collective-permute-start.8
  90.5 2.7 %collective-permute-start.11 = (f32[1792,128]{1,0:T(8,128)S(1)}, f32[1792,128]{1,0:T(8,128)S(1)}, u32[]{:S(2)}, u32[]{:S(2)}) collective-permute-start(f32[1792,128]{1,0:T(8,128)S(1)} %shard_map.95), channel_id=1, source_target_pairs={{0,4},{4,0},{1,5},{5,1},{2,6},{6,2},{3,7},{7,3},{8,12},{12,8},{9,1... | collective-permute-start | bytes 2752520 | tf_op jit(solution)/shard_map/ppermute | solution.py:41
  93.2 1.6 shard_map.92.near
  95.4 17.9 %all_to_all.37.parts = bf16[32,56,128]{2,1,0:T(8,128)(2,1)S(1)} all-to-all(bf16[32,56,128]{2,1,0:T(8,128)(2,1)S(1)} %shard_map.96), channel_id=1, replica_groups=mesh['y'=4,'z'=8,'core'=2,'samp'=4] {'y','z'}, dimensions={0} | all-to-all | bytes 917504 | tf_op jit(solution)/shard_map/all_to_all | solution.py:443
  113.6 19.7 %all_to_all.38.right = bf16[32,56,128]{2,1,0:T(8,128)(2,1)S(1)} all-to-all(bf16[32,56,128]{2,1,0:T(8,128)(2,1)S(1)} %get-tuple-element.67), channel_id=1, replica_groups=mesh['y'=4,'z'=8,'core'=2,'samp'=4] {'y','z'}, dimensions={0} | all-to-all | bytes 917504 | tf_op jit(solution)/shard_map/all_to_all | solution.py:443
  133.3 4.1 %collective-permute-start.12 = (bf16[32,56,128]{2,1,0:T(8,128)(2,1)S(1)}, bf16[32,56,128]{2,1,0:T(8,128)(2,1)S(1)}, u32[]{:S(2)}, u32[]{:S(2)}) collective-permute-start(bf16[32,56,128]{2,1,0:T(8,128)(2,1)S(1)} %all_to_all.38.right), channel_id=1, source_target_pairs={{0,4},{4,0},{1,5},{5,1},{2,6},{6,2},{3,7},{7,3},{8,12},{12,8},{9,1... | collective-permute-start | bytes 1376264 | tf_op jit(solution)/shard_map/ppermute | solution.py:41
  140.0 2.5 %collective-permute-start.15 = (f32[128,256]{1,0:T(8,128)S(1)}, f32[128,256]{1,0:T(8,128)S(1)}, u32[]{:S(2)}, u32[]{:S(2)}) collective-permute-start(f32[128,256]{1,0:T(8,128)S(1)} %get-tuple-element.71), channel_id=1, source_target_pairs={{0,2},{1,3},{2,0},{3,1},{4,6},{5,7},{6,4},{7,5},{8,10},{9,11},{10,... | collective-permute-start | bytes 393224 | tf_op jit(solution)/shard_map/ppermute | solution.py:41
  143.8 2.3 collective-permute-done.13.r1
  146.1 2.4 collective-permute-done.15.r3
  149.3 3.3 %collective-permute-start.16 = (f32[128,256]{1,0:T(8,128)S(1)}, f32[128,256]{1,0:T(8,128)S(1)}, u32[]{:S(2)}, u32[]{:S(2)}) collective-permute-start(f32[128,256]{1,0:T(8,128)S(1)} %get-tuple-element.75.c0.refs_0_), channel_id=1, source_target_pairs={{0,3},{1,0},{2,1},{3,2},{4,7},{5,4},{6,5},{7,6},{8,11},{9,8},{10,9... | collective-permute-start | bytes 393224 | tf_op jit(solution)/shard_map/ppermute | solution.py:41
  154.8 6.4 %collective-permute-done.18.c3.refs_1_ = f32[128,256]{1,0:T(8,128)S(1)} collective-permute-done((f32[128,256]{1,0:T(8,128)S(1)}, f32[128,256]{1,0:T(8,128)S(1)}, u32[]{:S(2)}, u32[]{:S(2)}) %collective-permute-start.18) | collective-permute-done | bytes 131104 | tf_op jit(solution)/shard_map/ppermute | solution.py:41
  164.6 1.6 shard_map.103.near
  166.8 18.2 %all_to_all.39.parts = bf16[32,56,128]{2,1,0:T(8,128)(2,1)S(1)} all-to-all(bf16[32,56,128]{2,1,0:T(8,128)(2,1)S(1)} %shard_map.107), channel_id=1, replica_groups=mesh['y'=4,'z'=8,'core'=2,'samp'=4] {'y','z'}, dimensions={0} | all-to-all | bytes 917504 | tf_op jit(solution)/shard_map/all_to_all | solution.py:443
  185.2 19.7 %all_to_all.40.right = bf16[32,56,128]{2,1,0:T(8,128)(2,1)S(1)} all-to-all(bf16[32,56,128]{2,1,0:T(8,128)(2,1)S(1)} %get-tuple-element.77), channel_id=1, replica_groups=mesh['y'=4,'z'=8,'core'=2,'samp'=4] {'y','z'}, dimensions={0} | all-to-all | bytes 917504 | tf_op jit(solution)/shard_map/all_to_all | solution.py:443
  204.9 4.1 %collective-permute-start.20 = (bf16[32,56,128]{2,1,0:T(8,128)(2,1)S(1)}, bf16[32,56,128]{2,1,0:T(8,128)(2,1)S(1)}, u32[]{:S(2)}, u32[]{:S(2)}) collective-permute-start(bf16[32,56,128]{2,1,0:T(8,128)(2,1)S(1)} %all_to_all.40.right), channel_id=1, source_target_pairs={{0,4},{4,0},{1,5},{5,1},{2,6},{6,2},{3,7},{7,3},{8,12},{12,8},{9,1... | collective-permute-start | bytes 1376264 | tf_op jit(solution)/shard_map/ppermute | solution.py:41
  213.1 2.3 collective-permute-start.22
  215.4 5.1 %collective-permute-done.21.r1 = f32[128,256]{1,0:T(8,128)S(1)} collective-permute-done((f32[128,256]{1,0:T(8,128)S(1)}, f32[128,256]{1,0:T(8,128)S(1)}, u32[]{:S(2)}, u32[]{:S(2)}) %collective-permute-start.21) | collective-permute-done | bytes 131104 | tf_op jit(solution)/shard_map/ppermute | solution.py:41
  221.5 9.3 %all-to-all-start.6 = ((f32[256,1,128]{2,1,0:T(1,128)}), f32[256,1,128]{2,1,0:T(1,128)S(1)}, u32[]{:S(2)}, u32[]{:S(2)}) async-start(f32[256,1,128]{2,1,0:T(1,128)} %bitcast.1), calls=%async_computation.6 | async-start | bytes 262144 | tf_op jit(solution)/shard_map/all_to_all | solution.py:505
  230.8 2.6 %collective-permute-start.24 = (f32[8,256]{1,0:T(8,128)S(1)}, f32[8,256]{1,0:T(8,128)S(1)}, u32[]{:S(2)}, u32[]{:S(2)}) collective-permute-start(f32[8,256]{1,0:T(8,128)S(1)} %get-tuple-element.88.n0), channel_id=1, source_target_pairs={{0,3},{1,0},{2,1},{3,2},{4,7},{5,4},{6,5},{7,6},{8,11},{9,8},{10,9... | collective-permute-start | bytes 24584 | tf_op jit(solution)/shard_map/ppermute | solution.py:41
  235.6 2.2 collective-permute-done.25.n2
  238.0 5.5 %all-to-all-done.6 = f32[256,1,128]{2,1,0:T(1,128)S(1)} async-done(((f32[256,1,128]{2,1,0:T(1,128)}), f32[256,1,128]{2,1,0:T(1,128)S(1)}, u32[]{:S(2)}, u32[]{:S(2)}) %all-to-all-start.6) | async-done | bytes 131104 | tf_op jit(solution)/shard_map/all_to_all | solution.py:505
  (65 shorter events, 37.4 us)
Async XLA Ops:
  0.6 5.3 %copy-start = (f32[1024,128]{1,0:T(8,128)S(1)}, f32[1024,128]{1,0:T(8,128)}, u32[]{:S(2)}) copy-start(f32[1024,128]{1,0:T(8,128)} %warm.3) | copy-start | bytes 1572868
  7.6 12.0 %collective-permute-start = (f32[1792,128]{1,0:T(8,128)S(1)}, f32[1792,128]{1,0:T(8,128)S(1)}, u32[]{:S(2)}, u32[]{:S(2)}) collective-permute-start(f32[1792,128]{1,0:T(8,128)S(1)} %shard_map.85), channel_id=1, source_target_pairs={{0,4},{4,0},{1,5},{5,1},{2,6},{6,2},{3,7},{7,3},{8,12},{12,8},{9,1... | collective-permute-start | bytes 2752520 | tf_op jit(solution)/shard_map/ppermute | solution.py:41
  10.8 6.3 %collective-permute-start.1 = (f32[136,256]{1,0:T(8,128)S(1)}, f32[136,256]{1,0:T(8,128)S(1)}, u32[]{:S(2)}, u32[]{:S(2)}) collective-permute-start(f32[136,256]{1,0:T(8,128)S(1)} %get-tuple-element.51), channel_id=1, source_target_pairs={{0,1},{1,2},{2,3},{3,0},{4,5},{5,6},{6,7},{7,4},{8,9},{9,10},{10,1... | collective-permute-start | bytes 417800 | tf_op jit(solution)/shard_map/ppermute | solution.py:41
  10.8 8.2 %collective-permute-start.2 = (f32[136,256]{1,0:T(8,128)S(1)}, f32[136,256]{1,0:T(8,128)S(1)}, u32[]{:S(2)}, u32[]{:S(2)}) collective-permute-start(f32[136,256]{1,0:T(8,128)S(1)} %get-tuple-element.52), channel_id=1, source_target_pairs={{0,3},{1,0},{2,1},{3,2},{4,7},{5,4},{6,5},{7,6},{8,11},{9,8},{10,9... | collective-permute-start | bytes 417800 | tf_op jit(solution)/shard_map/ppermute | solution.py:41
  13.5 6.1 %collective-permute-start.3 = (f32[136,256]{1,0:T(8,128)S(1)}, f32[136,256]{1,0:T(8,128)S(1)}, u32[]{:S(2)}, u32[]{:S(2)}) collective-permute-start(f32[136,256]{1,0:T(8,128)S(1)} %get-tuple-element.53), channel_id=1, source_target_pairs={{0,2},{1,3},{2,0},{3,1},{4,6},{5,7},{6,4},{7,5},{8,10},{9,11},{10,... | collective-permute-start | bytes 417800 | tf_op jit(solution)/shard_map/ppermute | solution.py:41
  64.7 6.1 %collective-permute-start.4 = (bf16[32,64,128]{2,1,0:T(8,128)(2,1)S(1)}, bf16[32,64,128]{2,1,0:T(8,128)(2,1)S(1)}, u32[]{:S(2)}, u32[]{:S(2)}) collective-permute-start(bf16[32,64,128]{2,1,0:T(8,128)(2,1)S(1)} %all_to_all.36.right.refs_0_), channel_id=1, source_target_pairs={{0,4},{4,0},{1,5},{5,1},{2,6},{6,2},{3,7},{7,3},{8,12},{12,8},{9,1... | collective-permute-start | bytes 1572872 | tf_op jit(solution)/shard_map/ppermute | solution.py:41
  70.6 10.9 %copy-start.1 = (s32[2,1024]{1,0:T(2,128)S(1)}, s32[2,1024]{1,0:T(2,128)}, u32[]{:S(2)}) copy-start(s32[2,1024]{1,0:T(2,128)} %mask.3) | copy-start | bytes 24580
  72.1 7.0 %collective-permute-start.5 = (f32[136,256]{1,0:T(8,128)S(1)}, f32[136,256]{1,0:T(8,128)S(1)}, u32[]{:S(2)}, u32[]{:S(2)}) collective-permute-start(f32[136,256]{1,0:T(8,128)S(1)} %get-tuple-element.59), channel_id=1, source_target_pairs={{0,1},{1,2},{2,3},{3,0},{4,5},{5,6},{6,7},{7,4},{8,9},{9,10},{10,1... | collective-permute-start | bytes 417800 | tf_op jit(solution)/shard_map/ppermute | solution.py:41
  72.7 7.6 %collective-permute-start.7 = (f32[136,256]{1,0:T(8,128)S(1)}, f32[136,256]{1,0:T(8,128)S(1)}, u32[]{:S(2)}, u32[]{:S(2)}) collective-permute-start(f32[136,256]{1,0:T(8,128)S(1)} %get-tuple-element.61), channel_id=1, source_target_pairs={{0,2},{1,3},{2,0},{3,1},{4,6},{5,7},{6,4},{7,5},{8,10},{9,11},{10,... | collective-permute-start | bytes 417800 | tf_op jit(solution)/shard_map/ppermute | solution.py:41
  75.1 6.3 %collective-permute-start.6 = (f32[136,256]{1,0:T(8,128)S(1)}, f32[136,256]{1,0:T(8,128)S(1)}, u32[]{:S(2)}, u32[]{:S(2)}) collective-permute-start(f32[136,256]{1,0:T(8,128)S(1)} %get-tuple-element.60), channel_id=1, source_target_pairs={{0,3},{1,0},{2,1},{3,2},{4,7},{5,4},{6,5},{7,6},{8,11},{9,8},{10,9... | collective-permute-start | bytes 417800 | tf_op jit(solution)/shard_map/ppermute | solution.py:41
  81.7 5.3 %collective-permute-start.10 = (bf16[128,256]{1,0:T(8,128)(2,1)S(1)}, bf16[128,256]{1,0:T(8,128)(2,1)S(1)}, u32[]{:S(2)}, u32[]{:S(2)}) collective-permute-start(bf16[128,256]{1,0:T(8,128)(2,1)S(1)} %get-tuple-element.65.c0.refs_0_), channel_id=1, source_target_pairs={{0,1},{1,2},{2,3},{3,0},{4,5},{5,6},{6,7},{7,4},{8,9},{9,10},{10,1... | collective-permute-start | bytes 196616 | tf_op jit(solution)/shard_map/ppermute | solution.py:41
  82.7 4.3 %collective-permute-start.8 = (bf16[128,256]{1,0:T(8,128)(2,1)S(1)}, bf16[128,256]{1,0:T(8,128)(2,1)S(1)}, u32[]{:S(2)}, u32[]{:S(2)}) collective-permute-start(bf16[128,256]{1,0:T(8,128)(2,1)S(1)} %get-tuple-element.65.c0.refs_0_), channel_id=1, source_target_pairs={{0,3},{1,0},{2,1},{3,2},{4,7},{5,4},{6,5},{7,6},{8,11},{9,8},{10,9... | collective-permute-start | bytes 196616 | tf_op jit(solution)/shard_map/ppermute | solution.py:41
  85.0 4.6 %collective-permute-start.9 = (bf16[128,256]{1,0:T(8,128)(2,1)S(1)}, bf16[128,256]{1,0:T(8,128)(2,1)S(1)}, u32[]{:S(2)}, u32[]{:S(2)}) collective-permute-start(bf16[128,256]{1,0:T(8,128)(2,1)S(1)} %get-tuple-element.65.c0.refs_0_), channel_id=1, source_target_pairs={{0,2},{1,3},{2,0},{3,1},{4,6},{5,7},{6,4},{7,5},{8,10},{9,11},{10,... | collective-permute-start | bytes 196616 | tf_op jit(solution)/shard_map/ppermute | solution.py:41
  90.5 4.8 %collective-permute-start.11 = (f32[1792,128]{1,0:T(8,128)S(1)}, f32[1792,128]{1,0:T(8,128)S(1)}, u32[]{:S(2)}, u32[]{:S(2)}) collective-permute-start(f32[1792,128]{1,0:T(8,128)S(1)} %shard_map.95), channel_id=1, source_target_pairs={{0,4},{4,0},{1,5},{5,1},{2,6},{6,2},{3,7},{7,3},{8,12},{12,8},{9,1... | collective-permute-start | bytes 2752520 | tf_op jit(solution)/shard_map/ppermute | solution.py:41
  133.3 5.6 %collective-permute-start.12 = (bf16[32,56,128]{2,1,0:T(8,128)(2,1)S(1)}, bf16[32,56,128]{2,1,0:T(8,128)(2,1)S(1)}, u32[]{:S(2)}, u32[]{:S(2)}) collective-permute-start(bf16[32,56,128]{2,1,0:T(8,128)(2,1)S(1)} %all_to_all.38.right), channel_id=1, source_target_pairs={{0,4},{4,0},{1,5},{5,1},{2,6},{6,2},{3,7},{7,3},{8,12},{12,8},{9,1... | collective-permute-start | bytes 1376264 | tf_op jit(solution)/shard_map/ppermute | solution.py:41
  139.9 6.2 %collective-permute-start.13 = (f32[128,256]{1,0:T(8,128)S(1)}, f32[128,256]{1,0:T(8,128)S(1)}, u32[]{:S(2)}, u32[]{:S(2)}) collective-permute-start(f32[128,256]{1,0:T(8,128)S(1)} %get-tuple-element.69), channel_id=1, source_target_pairs={{0,1},{1,2},{2,3},{3,0},{4,5},{5,6},{6,7},{7,4},{8,9},{9,10},{10,1... | collective-permute-start | bytes 393224 | tf_op jit(solution)/shard_map/ppermute | solution.py:41
  140.0 8.5 %collective-permute-start.15 = (f32[128,256]{1,0:T(8,128)S(1)}, f32[128,256]{1,0:T(8,128)S(1)}, u32[]{:S(2)}, u32[]{:S(2)}) collective-permute-start(f32[128,256]{1,0:T(8,128)S(1)} %get-tuple-element.71), channel_id=1, source_target_pairs={{0,2},{1,3},{2,0},{3,1},{4,6},{5,7},{6,4},{7,5},{8,10},{9,11},{10,... | collective-permute-start | bytes 393224 | tf_op jit(solution)/shard_map/ppermute | solution.py:41
  143.5 5.6 %collective-permute-start.14 = (f32[128,256]{1,0:T(8,128)S(1)}, f32[128,256]{1,0:T(8,128)S(1)}, u32[]{:S(2)}, u32[]{:S(2)}) collective-permute-start(f32[128,256]{1,0:T(8,128)S(1)} %get-tuple-element.70), channel_id=1, source_target_pairs={{0,3},{1,0},{2,1},{3,2},{4,7},{5,4},{6,5},{7,6},{8,11},{9,8},{10,9... | collective-permute-start | bytes 393224 | tf_op jit(solution)/shard_map/ppermute | solution.py:41
  149.3 5.5 %collective-permute-start.16 = (f32[128,256]{1,0:T(8,128)S(1)}, f32[128,256]{1,0:T(8,128)S(1)}, u32[]{:S(2)}, u32[]{:S(2)}) collective-permute-start(f32[128,256]{1,0:T(8,128)S(1)} %get-tuple-element.75.c0.refs_0_), channel_id=1, source_target_pairs={{0,3},{1,0},{2,1},{3,2},{4,7},{5,4},{6,5},{7,6},{8,11},{9,8},{10,9... | collective-permute-start | bytes 393224 | tf_op jit(solution)/shard_map/ppermute | solution.py:41
  152.6 8.7 %collective-permute-start.18 = (f32[128,256]{1,0:T(8,128)S(1)}, f32[128,256]{1,0:T(8,128)S(1)}, u32[]{:S(2)}, u32[]{:S(2)}) collective-permute-start(f32[128,256]{1,0:T(8,128)S(1)} %get-tuple-element.75.c0.refs_0_), channel_id=1, source_target_pairs={{0,1},{1,2},{2,3},{3,0},{4,5},{5,6},{6,7},{7,4},{8,9},{9,10},{10,1... | collective-permute-start | bytes 393224 | tf_op jit(solution)/shard_map/ppermute | solution.py:41
  152.6 9.8 %collective-permute-start.17 = (f32[128,256]{1,0:T(8,128)S(1)}, f32[128,256]{1,0:T(8,128)S(1)}, u32[]{:S(2)}, u32[]{:S(2)}) collective-permute-start(f32[128,256]{1,0:T(8,128)S(1)} %get-tuple-element.75.c0.refs_0_), channel_id=1, source_target_pairs={{0,2},{1,3},{2,0},{3,1},{4,6},{5,7},{6,4},{7,5},{8,10},{9,11},{10,... | collective-permute-start | bytes 393224 | tf_op jit(solution)/shard_map/ppermute | solution.py:41
  163.3 3.4 %collective-permute-start.19 = (f32[1792,128]{1,0:T(8,128)S(1)}, f32[1792,128]{1,0:T(8,128)S(1)}, u32[]{:S(2)}, u32[]{:S(2)}) collective-permute-start(f32[1792,128]{1,0:T(8,128)S(1)} %shard_map.106), channel_id=1, source_target_pairs={{0,4},{4,0},{1,5},{5,1},{2,6},{6,2},{3,7},{7,3},{8,12},{12,8},{9,1... | collective-permute-start | bytes 2752520 | tf_op jit(solution)/shard_map/ppermute | solution.py:41
  204.9 5.6 %collective-permute-start.20 = (bf16[32,56,128]{2,1,0:T(8,128)(2,1)S(1)}, bf16[32,56,128]{2,1,0:T(8,128)(2,1)S(1)}, u32[]{:S(2)}, u32[]{:S(2)}) collective-permute-start(bf16[32,56,128]{2,1,0:T(8,128)(2,1)S(1)} %all_to_all.40.right), channel_id=1, source_target_pairs={{0,4},{4,0},{1,5},{5,1},{2,6},{6,2},{3,7},{7,3},{8,12},{12,8},{9,1... | collective-permute-start | bytes 1376264 | tf_op jit(solution)/shard_map/ppermute | solution.py:41
  211.5 9.0 %collective-permute-start.21 = (f32[128,256]{1,0:T(8,128)S(1)}, f32[128,256]{1,0:T(8,128)S(1)}, u32[]{:S(2)}, u32[]{:S(2)}) collective-permute-start(f32[128,256]{1,0:T(8,128)S(1)} %get-tuple-element.79), channel_id=1, source_target_pairs={{0,1},{1,2},{2,3},{3,0},{4,5},{5,6},{6,7},{7,4},{8,9},{9,10},{10,1... | collective-permute-start | bytes 393224 | tf_op jit(solution)/shard_map/ppermute | solution.py:41
  211.6 8.9 %collective-permute-start.23 = (f32[128,256]{1,0:T(8,128)S(1)}, f32[128,256]{1,0:T(8,128)S(1)}, u32[]{:S(2)}, u32[]{:S(2)}) collective-permute-start(f32[128,256]{1,0:T(8,128)S(1)} %get-tuple-element.81), channel_id=1, source_target_pairs={{0,2},{1,3},{2,0},{3,1},{4,6},{5,7},{6,4},{7,5},{8,10},{9,11},{10,... | collective-permute-start | bytes 393224 | tf_op jit(solution)/shard_map/ppermute | solution.py:41
  213.1 7.5 %collective-permute-start.22 = (f32[128,256]{1,0:T(8,128)S(1)}, f32[128,256]{1,0:T(8,128)S(1)}, u32[]{:S(2)}, u32[]{:S(2)}) collective-permute-start(f32[128,256]{1,0:T(8,128)S(1)} %get-tuple-element.80), channel_id=1, source_target_pairs={{0,3},{1,0},{2,1},{3,2},{4,7},{5,4},{6,5},{7,6},{8,11},{9,8},{10,9... | collective-permute-start | bytes 393224 | tf_op jit(solution)/shard_map/ppermute | solution.py:41
  221.5 22.1 %all-to-all-start.6 = ((f32[256,1,128]{2,1,0:T(1,128)}), f32[256,1,128]{2,1,0:T(1,128)S(1)}, u32[]{:S(2)}, u32[]{:S(2)}) async-start(f32[256,1,128]{2,1,0:T(1,128)} %bitcast.1), calls=%async_computation.6 | async-start | bytes 262144 | tf_op jit(solution)/shard_map/all_to_all | solution.py:505
  230.8 4.8 %collective-permute-start.24 = (f32[8,256]{1,0:T(8,128)S(1)}, f32[8,256]{1,0:T(8,128)S(1)}, u32[]{:S(2)}, u32[]{:S(2)}) collective-permute-start(f32[8,256]{1,0:T(8,128)S(1)} %get-tuple-element.88.n0), channel_id=1, source_target_pairs={{0,3},{1,0},{2,1},{3,2},{4,7},{5,4},{6,5},{7,6},{8,11},{9,8},{10,9... | collective-permute-start | bytes 24584 | tf_op jit(solution)/shard_map/ppermute | solution.py:41
  233.4 4.3 %collective-permute-start.25 = (f32[8,256]{1,0:T(8,128)S(1)}, f32[8,256]{1,0:T(8,128)S(1)}, u32[]{:S(2)}, u32[]{:S(2)}) collective-permute-start(f32[8,256]{1,0:T(8,128)S(1)} %get-tuple-element.88.n0), channel_id=1, source_target_pairs={{0,2},{1,3},{2,0},{3,1},{4,6},{5,7},{6,4},{7,5},{8,10},{9,11},{10,... | collective-permute-start | bytes 24584 | tf_op jit(solution)/shard_map/ppermute | solution.py:41
  234.0 4.0 %collective-permute-start.26 = (f32[8,256]{1,0:T(8,128)S(1)}, f32[8,256]{1,0:T(8,128)S(1)}, u32[]{:S(2)}, u32[]{:S(2)}) collective-permute-start(f32[8,256]{1,0:T(8,128)S(1)} %get-tuple-element.88.n0), channel_id=1, source_target_pairs={{0,1},{1,2},{2,3},{3,0},{4,5},{5,6},{6,7},{7,4},{8,9},{9,10},{10,1... | collective-permute-start | bytes 24584 | tf_op jit(solution)/shard_map/ppermute | solution.py:41

commit v2 on v0

--- a/solution.py
+++ b/solution.py
@@ -9,6 +9,7 @@
 
 ITERS = 2
 FEAT = ("y", "z", "core")
+ALL = ("y", "z", "core", "samp")
 PLANE = ("y", "z")
 BF = jnp.bfloat16
 F32 = jnp.float32
@@ -62,6 +63,16 @@
     return pl.multiple_of(((lax.axis_index("samp") + k) & 3) * width, width)
 
 
+def thirds(value, rows):
+    value = jnp.broadcast_to(value, (rows, value.shape[1]))
+    high = value.astype(BF).astype(F32)
+    middle = (value - high).astype(BF).astype(F32)
+    low = (value - high) - middle
+    which = lax.broadcasted_iota(jnp.int32, value.shape, 0)
+    spread = jnp.where(which == 0, high, jnp.where(which == 1, middle, low))
+    return jnp.where(which < 3, spread, 0.0)
+
+
 def corr_first(design, targets, step, block):
     rows, cols = design.shape
     tasks = targets.shape[1]
@@ -106,14 +117,16 @@
         mine.wait()
         for k, out in enumerate((o0, o1, o2, o3)):
             at = block_at(k, width)
-            out[:tasks, :] = total[:, pl.ds(at, width)]
-            out[tasks:, :] = squares[:, pl.ds(at, width)]
+            out[:tasks, :] = total[:, pl.ds(at, width)].astype(out.dtype)
+            row = jnp.sum(squares[:, pl.ds(at, width)], axis=0, keepdims=True)
+            out[tasks:, :] = thirds(row, 2 * EXTRA).astype(out.dtype)
 
     hbm = pl.BlockSpec(memory_space=pltpu.HBM)
     return pl.pallas_call(
         body,
         out_shape=(
-            *[shape_of((tasks + 8, width))] * 4,
+            shape_of((tasks + 2 * EXTRA, width)),
+            *[shape_of((tasks + 2 * EXTRA, width), BF)] * 3,
             pltpu.VMEM(design.shape, design.dtype),
             shape_of((block, tasks), targets.dtype),
         ),
@@ -189,7 +202,9 @@
         out[...] = total.reshape(out.shape).astype(BF)
         if corr:
             c0, c1, c2, c3, _, steps, top = refs
-            both = c0[...] + c1[...] + c2[...] + c3[...]
+            both = c0[...]
+            for share in (c1, c2, c3):
+                both += share[...].astype(F32)
             column_squares = jnp.sum(both[tasks:], axis=0, keepdims=True)
             steps[...] = 0.5 / (1.0 + column_squares)
             top[...] = jnp.full(top.shape, jnp.max(lane_norms(both[:tasks])), F32)
@@ -230,7 +245,7 @@
     return jnp.max(jnp.sum(pieces, axis=1))
 
 
-def grad_far(design, right, start, block, near=None):
+def grad_far(design, right, start, block, near=None, sent_as=F32):
     tasks, cols = start.shape
     width = cols // 4
     extra = 0 if near is None else EXTRA
@@ -241,13 +256,14 @@
         grad_loop(False, right, design, total, block)
         for k, out in enumerate(outs):
             at = block_at(k, width)
-            out[:tasks, :] = total[:, pl.ds(at, width)]
+            out[:tasks, :] = total[:, pl.ds(at, width)].astype(out.dtype)
         if extra:
             top = jnp.maximum(top_of(right, block), top_of(refs[0], block))
             for out in outs:
                 out[tasks:, :] = jnp.full((extra, width), top, F32)
 
-    outs = [shape_of((tasks + extra, width))] * 4
+    outs = [shape_of((tasks + extra, width))]
+    outs += [shape_of((tasks + extra, width), sent_as)] * 3
     args = [design, right, start] + ([] if near is None else [near])
     return call(body, outs, *args, scratch=[pltpu.VMEM((tasks, cols), F32)])
 
@@ -327,28 +343,19 @@
     return call(body, outs, *args, smem=(7,))
 
 
-def last_norms(parts, current, stats, n0, n1, at):
-    width = n0.shape[1]
-
-    def body(own, r1, r2, r3, current, stats, n0, n1, out):
-        norms = lane_norms(own[...] + r1[...] + r2[...] + r3[...])
+def last_norms(parts, current, stats, n0, n1, at, devices):
+    def body(own, r1, r2, r3, current, stats, n0, n1, norms_out, copies):
+        gradient = own[...]
+        for share in (r1, r2, r3):
+            gradient += share[...].astype(F32)
+        norms = lane_norms(gradient)
+        norms_out[...] = jnp.concatenate([n0[...], n1[...], norms] + [norms] * 5, axis=0)
         row = lane(stats[...], at + 2, jnp.sum(lane_norms(current[...])))
         row = lane(row, at + 3, jnp.max(norms))
-        wide = jnp.concatenate([row] * (width // row.shape[1]), axis=1)
-        out[...] = jnp.concatenate([n0[...], n1[...], norms] + [wide] * 5, axis=0)
-
-    return call(body, shape_of((8, width)), *parts, current, stats, n0, n1)
-
-
-def of_samples(blocks, copies):
-    def body(own, n1, n2, n3, out):
-        rows = [ref[3:4, 0:128] for ref in (own, n1, n2, n3)]
-        total = (rows[0] + rows[2]) + (rows[1] + rows[3])
-        high = jnp.maximum(jnp.maximum(rows[0], rows[2]), jnp.maximum(rows[1], rows[3]))
-        at = lax.broadcasted_iota(jnp.int32, total.shape, 1)
-        out[...] = jnp.broadcast_to(jnp.where((at & 7) == 3, high, total), out.shape)
-
-    return call(body, shape_of((copies, 128)), *blocks)
+        copies[...] = jnp.broadcast_to(row, copies.shape)
+
+    outs = [shape_of((8, n0.shape[1])), shape_of((devices, stats.shape[1]))]
+    return call(body, outs, *parts, current, stats, n0, n1)
 
 
 def finish(everyone, tops, index, blocks):
@@ -416,6 +423,10 @@
     planes = lax.axis_size("y") * lax.axis_size("z")
     block = half // planes
     step = 8 * block
+    devices = 1
+    for axis in ALL:
+        devices *= lax.axis_size(axis)
+
     blocks = tops = stats = None
     norms = []
     for t in range(ITERS + 1):
@@ -437,7 +448,10 @@
         far_rows = shifted(near_rows, "core", 1)
         grad = grad_near(design, near_rows, block)
         shares = to_owners(
-            grad_far(design, far_rows, grad, block, near_rows if t == 0 else None)
+            grad_far(
+                design, far_rows, grad, block, near_rows if t == 0 else None,
+                F32 if t < ITERS else BF,
+            )
         )
         if t < ITERS:
             current, sent, own_norms, stats, tops = prox(
@@ -449,11 +463,9 @@
             if t + 1 == ITERS:
                 coefficients = turned_back(blocks)
         else:
-            packed = last_norms(shares, current, stats, *norms, 8 * t)
+            packed, copies = last_norms(shares, current, stats, *norms, 8 * t, devices)
     norm_blocks = from_owners(packed)
-    features = planes * lax.axis_size("core")
-    copies = of_samples(norm_blocks, features)
-    everyone = lax.all_to_all(copies[:, None, :], FEAT, split_axis=0, concat_axis=0, tiled=True)
+    everyone = lax.all_to_all(copies[:, None, :], ALL, split_axis=0, concat_axis=0, tiled=True)
     correlations, gaps, counts = finish(
         everyone.reshape(copies.shape), tops, penalty_index, norm_blocks
     )

time: 245 us -> 238 us (0.971)
  blocking collectives: 120 us -> 116 us
  waiting for transfers between devices: 41.2 us -> 37.7 us
    all_to_all x6, blocking collectives: 120 us -> 116 us  [plane_exchange(): lax.all_to_all(blocks, PLANE, split_axis=0, concat_axis=0, tiled=True)]
    all_to_all x1, waiting for transfers between devices: 8.31 us -> 5.52 us  [local(): lax.all_to_all(copies[:, None, :], ALL, split_axis=0, concat_axis=0, tile...]
    pallas_call x24 -> x23, Pallas kernels: 22.4 us -> 22.4 us  [call(): pl.pallas_call(body, out_shape=shapes[0] if single else tuple(shapes), in...]
  transfers between devices with their start and end apart: 28 -> 28, of which waited for: 24 -> 25; matrix products, arithmetic and copies ran while one was open for 0% -> 0% of each run, Pallas kernels for 4% -> 4%
where the time goes in v2:
time: 238 us
  blocking collectives  116 us (49%)
  starting transfers between devices  54.7 us (23%)
  waiting for transfers between devices  37.7 us (16%)
  Pallas kernels  27.7 us (12%)
    all_to_all x6, blocking collectives, plane_exchange(): lax.all_to_all(blocks, PLANE, split_axis=0, concat_axis=0, tiled=True)  116 us
    ppermute x27, starting transfers between devices, shifted(): return lax.ppermute(value, axis, [(i, (i + by) % n) for i in range(n)])  46.8 us
    ppermute x27, waiting for transfers between devices, shifted(): return lax.ppermute(value, axis, [(i, (i + by) % n) for i in range(n)])  32.2 us
    pallas_call x23, Pallas kernels, call(): pl.pallas_call(body, out_shape=shapes[0] if single else tuple(shapes), in...  22.4 us
    all_to_all x1, starting transfers between devices, local(): lax.all_to_all(copies[:, None, :], ALL, split_axis=0, concat_axis=0, tile...  7.92 us
    all_to_all x1, waiting for transfers between devices, local(): lax.all_to_all(copies[:, None, :], ALL, split_axis=0, concat_axis=0, tile...  5.52 us
    pallas_call x1, Pallas kernels, corr_first(): pl.pallas_call(body, out_shape=(shape_of((tasks + 2 * EXTRA, width)), *[s...  5.3 us
  transfers between devices with their start and end apart: 28, of which 25 were waited for; matrix products, arithmetic and copies ran while one was open for 0% of the time, Pallas kernels for 4%

profile of v2, /device:TPU:1, one launch (start us, length us, event | category | flops | bytes accessed | tf_op | source)
XLA Modules:
  0.0 237.7 jit_solution(10337924713701100061)
XLA Ops:
  0.6 5.3 %corr_first.1 = (f32[144,256]{1,0:T(8,128)S(1)}, bf16[144,256]{1,0:T(8,128)(2,1)S(1)}, bf16[144,256]{1,0:T(8,128)(2,1)S(1)}, bf16[144,256]{1,0:T(8,128)(2,1)S(1)...) custom-call(bf16[3584,1024]{1,0:T(8,128)(2,1)} %design.1, bf16[3584,128]{1,0:T(8,128)(2,1)} %targets.1), custom_call_target="tpu_custom_call" | custom-call | tf_op jit(solution)/shard_map/corr_first/pallas_call | solution.py:125
  6.0 1.7 shard_map.85
  7.6 3.3 %collective-permute-start = (f32[1792,128]{1,0:T(8,128)S(1)}, f32[1792,128]{1,0:T(8,128)S(1)}, u32[]{:S(2)}, u32[]{:S(2)}) collective-permute-start(f32[1792,128]{1,0:T(8,128)S(1)} %shard_map.85), channel_id=1, source_target_pairs={{0,4},{4,0},{1,5},{5,1},{2,6},{6,2},{3,7},{7,3},{8,12},{12,8},{9,1... | collective-permute-start | bytes 2752520 | tf_op jit(solution)/shard_map/ppermute | solution.py:41
  10.9 2.7 %collective-permute-start.2 = (bf16[144,256]{1,0:T(8,128)(2,1)S(1)}, bf16[144,256]{1,0:T(8,128)(2,1)S(1)}, u32[]{:S(2)}, u32[]{:S(2)}) collective-permute-start(bf16[144,256]{1,0:T(8,128)(2,1)S(1)} %get-tuple-element.52), channel_id=1, source_target_pairs={{0,3},{1,0},{2,1},{3,2},{4,7},{5,4},{6,5},{7,6},{8,11},{9,8},{10,9... | collective-permute-start | bytes 221192 | tf_op jit(solution)/shard_map/ppermute | solution.py:41
  13.6 1.8 shard_map.84
  18.6 21.1 %all_to_all.35.parts = bf16[32,56,128]{2,1,0:T(8,128)(2,1)S(1)} all-to-all(bf16[32,56,128]{2,1,0:T(8,128)(2,1)S(1)} %get-tuple-element.54), channel_id=1, replica_groups=mesh['y'=4,'z'=8,'core'=2,'samp'=4] {'y','z'}, dimensions={0} | all-to-all | bytes 917504 | tf_op jit(solution)/shard_map/all_to_all | solution.py:417
  39.9 19.2 %all_to_all.36.right.refs_0_ = bf16[32,64,128]{2,1,0:T(8,128)(2,1)S(1)} all-to-all(bf16[32,64,128]{2,1,0:T(8,128)(2,1)S(1)} %get-tuple-element.57), channel_id=1, replica_groups=mesh['y'=4,'z'=8,'core'=2,'samp'=4] {'y','z'}, dimensions={0} | all-to-all | bytes 1048576 | tf_op jit(solution)/shard_map/all_to_all | solution.py:417
  59.1 5.4 %collective-permute-start.4 = (bf16[32,64,128]{2,1,0:T(8,128)(2,1)S(1)}, bf16[32,64,128]{2,1,0:T(8,128)(2,1)S(1)}, u32[]{:S(2)}, u32[]{:S(2)}) collective-permute-start(bf16[32,64,128]{2,1,0:T(8,128)(2,1)S(1)} %all_to_all.36.right.refs_0_), channel_id=1, source_target_pairs={{0,4},{4,0},{1,5},{5,1},{2,6},{6,2},{3,7},{7,3},{8,12},{12,8},{9,1... | collective-permute-start | bytes 1572872 | tf_op jit(solution)/shard_map/ppermute | solution.py:41
  67.6 2.9 %collective-permute-start.5 = (f32[136,256]{1,0:T(8,128)S(1)}, f32[136,256]{1,0:T(8,128)S(1)}, u32[]{:S(2)}, u32[]{:S(2)}) collective-permute-start(f32[136,256]{1,0:T(8,128)S(1)} %get-tuple-element.59), channel_id=1, source_target_pairs={{0,1},{1,2},{2,3},{3,0},{4,5},{5,6},{6,7},{7,4},{8,9},{9,10},{10,1... | collective-permute-start | bytes 417800 | tf_op jit(solution)/shard_map/ppermute | solution.py:41
  70.6 1.9 collective-permute-start.7
  78.2 2.7 %collective-permute-start.8 = (bf16[128,256]{1,0:T(8,128)(2,1)S(1)}, bf16[128,256]{1,0:T(8,128)(2,1)S(1)}, u32[]{:S(2)}, u32[]{:S(2)}) collective-permute-start(bf16[128,256]{1,0:T(8,128)(2,1)S(1)} %get-tuple-element.65.c0), channel_id=1, source_target_pairs={{0,3},{1,0},{2,1},{3,2},{4,7},{5,4},{6,5},{7,6},{8,11},{9,8},{10,9... | collective-permute-start | bytes 196616 | tf_op jit(solution)/shard_map/ppermute | solution.py:41
  82.4 3.7 %collective-permute-done.9.c2 = bf16[128,256]{1,0:T(8,128)(2,1)S(1)} collective-permute-done((bf16[128,256]{1,0:T(8,128)(2,1)S(1)}, bf16[128,256]{1,0:T(8,128)(2,1)S(1)}, u32[]{:S(2)}, u32[]{:S(2)}) %collective-permute-start.9) | collective-permute-done | bytes 65568 | tf_op jit(solution)/shard_map/ppermute | solution.py:41
  87.8 2.4 %collective-permute-start.11 = (f32[1792,128]{1,0:T(8,128)S(1)}, f32[1792,128]{1,0:T(8,128)S(1)}, u32[]{:S(2)}, u32[]{:S(2)}) collective-permute-start(f32[1792,128]{1,0:T(8,128)S(1)} %shard_map.92), channel_id=1, source_target_pairs={{0,4},{4,0},{1,5},{5,1},{2,6},{6,2},{3,7},{7,3},{8,12},{12,8},{9,1... | collective-permute-start | bytes 2752520 | tf_op jit(solution)/shard_map/ppermute | solution.py:41
  92.3 18.0 %all_to_all.37.parts = bf16[32,56,128]{2,1,0:T(8,128)(2,1)S(1)} all-to-all(bf16[32,56,128]{2,1,0:T(8,128)(2,1)S(1)} %shard_map.93), channel_id=1, replica_groups=mesh['y'=4,'z'=8,'core'=2,'samp'=4] {'y','z'}, dimensions={0} | all-to-all | bytes 917504 | tf_op jit(solution)/shard_map/all_to_all | solution.py:417
  110.5 19.7 %all_to_all.38.right = bf16[32,56,128]{2,1,0:T(8,128)(2,1)S(1)} all-to-all(bf16[32,56,128]{2,1,0:T(8,128)(2,1)S(1)} %get-tuple-element.67), channel_id=1, replica_groups=mesh['y'=4,'z'=8,'core'=2,'samp'=4] {'y','z'}, dimensions={0} | all-to-all | bytes 917504 | tf_op jit(solution)/shard_map/all_to_all | solution.py:417
  130.3 4.1 %collective-permute-start.12 = (bf16[32,56,128]{2,1,0:T(8,128)(2,1)S(1)}, bf16[32,56,128]{2,1,0:T(8,128)(2,1)S(1)}, u32[]{:S(2)}, u32[]{:S(2)}) collective-permute-start(bf16[32,56,128]{2,1,0:T(8,128)(2,1)S(1)} %all_to_all.38.right), channel_id=1, source_target_pairs={{0,4},{4,0},{1,5},{5,1},{2,6},{6,2},{3,7},{7,3},{8,12},{12,8},{9,1... | collective-permute-start | bytes 1376264 | tf_op jit(solution)/shard_map/ppermute | solution.py:41
  137.3 2.7 %collective-permute-start.14 = (f32[128,256]{1,0:T(8,128)S(1)}, f32[128,256]{1,0:T(8,128)S(1)}, u32[]{:S(2)}, u32[]{:S(2)}) collective-permute-start(f32[128,256]{1,0:T(8,128)S(1)} %get-tuple-element.70), channel_id=1, source_target_pairs={{0,3},{1,0},{2,1},{3,2},{4,7},{5,4},{6,5},{7,6},{8,11},{9,8},{10,9... | collective-permute-start | bytes 393224 | tf_op jit(solution)/shard_map/ppermute | solution.py:41
  140.1 3.0 %collective-permute-done.13.r1 = f32[128,256]{1,0:T(8,128)S(1)} collective-permute-done((f32[128,256]{1,0:T(8,128)S(1)}, f32[128,256]{1,0:T(8,128)S(1)}, u32[]{:S(2)}, u32[]{:S(2)}) %collective-permute-start.13) | collective-permute-done | bytes 131104 | tf_op jit(solution)/shard_map/ppermute | solution.py:41
  143.2 1.8 collective-permute-done.14.r2
  145.8 3.0 %collective-permute-start.16 = (f32[128,256]{1,0:T(8,128)S(1)}, f32[128,256]{1,0:T(8,128)S(1)}, u32[]{:S(2)}, u32[]{:S(2)}) collective-permute-start(f32[128,256]{1,0:T(8,128)S(1)} %get-tuple-element.75.c0), channel_id=1, source_target_pairs={{0,3},{1,0},{2,1},{3,2},{4,7},{5,4},{6,5},{7,6},{8,11},{9,8},{10,9... | collective-permute-start | bytes 393224 | tf_op jit(solution)/shard_map/ppermute | solution.py:41
  149.5 2.5 %collective-permute-done.16.c1 = f32[128,256]{1,0:T(8,128)S(1)} collective-permute-done((f32[128,256]{1,0:T(8,128)S(1)}, f32[128,256]{1,0:T(8,128)S(1)}, u32[]{:S(2)}, u32[]{:S(2)}) %collective-permute-start.16) | collective-permute-done | bytes 131104 | tf_op jit(solution)/shard_map/ppermute | solution.py:41
  152.0 2.2 collective-permute-done.17.c2
  154.3 3.1 %collective-permute-done.18.c3 = f32[128,256]{1,0:T(8,128)S(1)} collective-permute-done((f32[128,256]{1,0:T(8,128)S(1)}, f32[128,256]{1,0:T(8,128)S(1)}, u32[]{:S(2)}, u32[]{:S(2)}) %collective-permute-start.18) | collective-permute-done | bytes 131104 | tf_op jit(solution)/shard_map/ppermute | solution.py:41
  162.7 18.2 %all_to_all.39.parts = bf16[32,56,128]{2,1,0:T(8,128)(2,1)S(1)} all-to-all(bf16[32,56,128]{2,1,0:T(8,128)(2,1)S(1)} %shard_map.101), channel_id=1, replica_groups=mesh['y'=4,'z'=8,'core'=2,'samp'=4] {'y','z'}, dimensions={0} | all-to-all | bytes 917504 | tf_op jit(solution)/shard_map/all_to_all | solution.py:417
  181.1 19.7 %all_to_all.40.right = bf16[32,56,128]{2,1,0:T(8,128)(2,1)S(1)} all-to-all(bf16[32,56,128]{2,1,0:T(8,128)(2,1)S(1)} %get-tuple-element.77), channel_id=1, replica_groups=mesh['y'=4,'z'=8,'core'=2,'samp'=4] {'y','z'}, dimensions={0} | all-to-all | bytes 917504 | tf_op jit(solution)/shard_map/all_to_all | solution.py:417
  200.8 4.1 %collective-permute-start.20 = (bf16[32,56,128]{2,1,0:T(8,128)(2,1)S(1)}, bf16[32,56,128]{2,1,0:T(8,128)(2,1)S(1)}, u32[]{:S(2)}, u32[]{:S(2)}) collective-permute-start(bf16[32,56,128]{2,1,0:T(8,128)(2,1)S(1)} %all_to_all.40.right), channel_id=1, source_target_pairs={{0,4},{4,0},{1,5},{5,1},{2,6},{6,2},{3,7},{7,3},{8,12},{12,8},{9,1... | collective-permute-start | bytes 1376264 | tf_op jit(solution)/shard_map/ppermute | solution.py:41
  207.9 2.7 %collective-permute-start.22 = (bf16[128,256]{1,0:T(8,128)(2,1)S(1)}, bf16[128,256]{1,0:T(8,128)(2,1)S(1)}, u32[]{:S(2)}, u32[]{:S(2)}) collective-permute-start(bf16[128,256]{1,0:T(8,128)(2,1)S(1)} %get-tuple-element.80), channel_id=1, source_target_pairs={{0,3},{1,0},{2,1},{3,2},{4,7},{5,4},{6,5},{7,6},{8,11},{9,8},{10,9... | collective-permute-start | bytes 196616 | tf_op jit(solution)/shard_map/ppermute | solution.py:41
  212.6 2.6 %collective-permute-done.23.r3 = bf16[128,256]{1,0:T(8,128)(2,1)S(1)} collective-permute-done((bf16[128,256]{1,0:T(8,128)(2,1)S(1)}, bf16[128,256]{1,0:T(8,128)(2,1)S(1)}, u32[]{:S(2)}, u32[]{:S(2)}) %collective-permute-start.23) | collective-permute-done | bytes 65568 | tf_op jit(solution)/shard_map/ppermute | solution.py:41
  216.0 7.9 %all-to-all-start.6 = ((f32[256,1,128]{2,1,0:T(1,128)}), f32[256,1,128]{2,1,0:T(1,128)S(1)}, u32[]{:S(2)}, u32[]{:S(2)}) async-start(f32[256,1,128]{2,1,0:T(1,128)} %bitcast.1), calls=%async_computation.6 | async-start | bytes 262144 | tf_op jit(solution)/shard_map/all_to_all | solution.py:468
  224.0 2.6 %collective-permute-start.24 = (f32[8,256]{1,0:T(8,128)S(1)}, f32[8,256]{1,0:T(8,128)S(1)}, u32[]{:S(2)}, u32[]{:S(2)}) collective-permute-start(f32[8,256]{1,0:T(8,128)S(1)} %get-tuple-element.88.n0), channel_id=1, source_target_pairs={{0,3},{1,0},{2,1},{3,2},{4,7},{5,4},{6,5},{7,6},{8,11},{9,8},{10,9... | collective-permute-start | bytes 24584 | tf_op jit(solution)/shard_map/ppermute | solution.py:41
  228.7 2.2 collective-permute-done.25.n2
  231.2 5.5 %all-to-all-done.6 = f32[256,1,128]{2,1,0:T(1,128)S(1)} async-done(((f32[256,1,128]{2,1,0:T(1,128)}), f32[256,1,128]{2,1,0:T(1,128)S(1)}, u32[]{:S(2)}, u32[]{:S(2)}) %all-to-all-start.6) | async-done | bytes 131104 | tf_op jit(solution)/shard_map/all_to_all | solution.py:468
  (58 shorter events, 36.3 us)
Async XLA Ops:
  0.6 5.3 %copy-start = (f32[1024,128]{1,0:T(8,128)S(1)}, f32[1024,128]{1,0:T(8,128)}, u32[]{:S(2)}) copy-start(f32[1024,128]{1,0:T(8,128)} %warm.3) | copy-start | bytes 1572868
  7.6 10.7 %collective-permute-start = (f32[1792,128]{1,0:T(8,128)S(1)}, f32[1792,128]{1,0:T(8,128)S(1)}, u32[]{:S(2)}, u32[]{:S(2)}) collective-permute-start(f32[1792,128]{1,0:T(8,128)S(1)} %shard_map.85), channel_id=1, source_target_pairs={{0,4},{4,0},{1,5},{5,1},{2,6},{6,2},{3,7},{7,3},{8,12},{12,8},{9,1... | collective-permute-start | bytes 2752520 | tf_op jit(solution)/shard_map/ppermute | solution.py:41
  10.9 4.9 %collective-permute-start.1 = (bf16[144,256]{1,0:T(8,128)(2,1)S(1)}, bf16[144,256]{1,0:T(8,128)(2,1)S(1)}, u32[]{:S(2)}, u32[]{:S(2)}) collective-permute-start(bf16[144,256]{1,0:T(8,128)(2,1)S(1)} %get-tuple-element.51), channel_id=1, source_target_pairs={{0,1},{1,2},{2,3},{3,0},{4,5},{5,6},{6,7},{7,4},{8,9},{9,10},{10,1... | collective-permute-start | bytes 221192 | tf_op jit(solution)/shard_map/ppermute | solution.py:41
  10.9 5.8 %collective-permute-start.2 = (bf16[144,256]{1,0:T(8,128)(2,1)S(1)}, bf16[144,256]{1,0:T(8,128)(2,1)S(1)}, u32[]{:S(2)}, u32[]{:S(2)}) collective-permute-start(bf16[144,256]{1,0:T(8,128)(2,1)S(1)} %get-tuple-element.52), channel_id=1, source_target_pairs={{0,3},{1,0},{2,1},{3,2},{4,7},{5,4},{6,5},{7,6},{8,11},{9,8},{10,9... | collective-permute-start | bytes 221192 | tf_op jit(solution)/shard_map/ppermute | solution.py:41
  13.6 4.7 %collective-permute-start.3 = (bf16[144,256]{1,0:T(8,128)(2,1)S(1)}, bf16[144,256]{1,0:T(8,128)(2,1)S(1)}, u32[]{:S(2)}, u32[]{:S(2)}) collective-permute-start(bf16[144,256]{1,0:T(8,128)(2,1)S(1)} %get-tuple-element.53), channel_id=1, source_target_pairs={{0,2},{1,3},{2,0},{3,1},{4,6},{5,7},{6,4},{7,5},{8,10},{9,11},{10,... | collective-permute-start | bytes 221192 | tf_op jit(solution)/shard_map/ppermute | solution.py:41
  59.1 17.4 %copy-start.1 = (s32[2,1024]{1,0:T(2,128)S(1)}, s32[2,1024]{1,0:T(2,128)}, u32[]{:S(2)}) copy-start(s32[2,1024]{1,0:T(2,128)} %mask.3) | copy-start | bytes 24580
  59.1 6.9 %collective-permute-start.4 = (bf16[32,64,128]{2,1,0:T(8,128)(2,1)S(1)}, bf16[32,64,128]{2,1,0:T(8,128)(2,1)S(1)}, u32[]{:S(2)}, u32[]{:S(2)}) collective-permute-start(bf16[32,64,128]{2,1,0:T(8,128)(2,1)S(1)} %all_to_all.36.right.refs_0_), channel_id=1, source_target_pairs={{0,4},{4,0},{1,5},{5,1},{2,6},{6,2},{3,7},{7,3},{8,12},{12,8},{9,1... | collective-permute-start | bytes 1572872 | tf_op jit(solution)/shard_map/ppermute | solution.py:41
  67.6 6.1 %collective-permute-start.5 = (f32[136,256]{1,0:T(8,128)S(1)}, f32[136,256]{1,0:T(8,128)S(1)}, u32[]{:S(2)}, u32[]{:S(2)}) collective-permute-start(f32[136,256]{1,0:T(8,128)S(1)} %get-tuple-element.59), channel_id=1, source_target_pairs={{0,1},{1,2},{2,3},{3,0},{4,5},{5,6},{6,7},{7,4},{8,9},{9,10},{10,1... | collective-permute-start | bytes 417800 | tf_op jit(solution)/shard_map/ppermute | solution.py:41
  70.5 4.6 %collective-permute-start.6 = (f32[136,256]{1,0:T(8,128)S(1)}, f32[136,256]{1,0:T(8,128)S(1)}, u32[]{:S(2)}, u32[]{:S(2)}) collective-permute-start(f32[136,256]{1,0:T(8,128)S(1)} %get-tuple-element.60), channel_id=1, source_target_pairs={{0,3},{1,0},{2,1},{3,2},{4,7},{5,4},{6,5},{7,6},{8,11},{9,8},{10,9... | collective-permute-start | bytes 417800 | tf_op jit(solution)/shard_map/ppermute | solution.py:41
  70.6 6.0 %collective-permute-start.7 = (f32[136,256]{1,0:T(8,128)S(1)}, f32[136,256]{1,0:T(8,128)S(1)}, u32[]{:S(2)}, u32[]{:S(2)}) collective-permute-start(f32[136,256]{1,0:T(8,128)S(1)} %get-tuple-element.61), channel_id=1, source_target_pairs={{0,2},{1,3},{2,0},{3,1},{4,6},{5,7},{6,4},{7,5},{8,10},{9,11},{10,... | collective-permute-start | bytes 417800 | tf_op jit(solution)/shard_map/ppermute | solution.py:41
  76.7 5.7 %collective-permute-start.10 = (bf16[128,256]{1,0:T(8,128)(2,1)S(1)}, bf16[128,256]{1,0:T(8,128)(2,1)S(1)}, u32[]{:S(2)}, u32[]{:S(2)}) collective-permute-start(bf16[128,256]{1,0:T(8,128)(2,1)S(1)} %get-tuple-element.65.c0), channel_id=1, source_target_pairs={{0,1},{1,2},{2,3},{3,0},{4,5},{5,6},{6,7},{7,4},{8,9},{9,10},{10,1... | collective-permute-start | bytes 196616 | tf_op jit(solution)/shard_map/ppermute | solution.py:41
  78.2 4.3 %collective-permute-start.8 = (bf16[128,256]{1,0:T(8,128)(2,1)S(1)}, bf16[128,256]{1,0:T(8,128)(2,1)S(1)}, u32[]{:S(2)}, u32[]{:S(2)}) collective-permute-start(bf16[128,256]{1,0:T(8,128)(2,1)S(1)} %get-tuple-element.65.c0), channel_id=1, source_target_pairs={{0,3},{1,0},{2,1},{3,2},{4,7},{5,4},{6,5},{7,6},{8,11},{9,8},{10,9... | collective-permute-start | bytes 196616 | tf_op jit(solution)/shard_map/ppermute | solution.py:41
  80.9 5.2 %collective-permute-start.9 = (bf16[128,256]{1,0:T(8,128)(2,1)S(1)}, bf16[128,256]{1,0:T(8,128)(2,1)S(1)}, u32[]{:S(2)}, u32[]{:S(2)}) collective-permute-start(bf16[128,256]{1,0:T(8,128)(2,1)S(1)} %get-tuple-element.65.c0), channel_id=1, source_target_pairs={{0,2},{1,3},{2,0},{3,1},{4,6},{5,7},{6,4},{7,5},{8,10},{9,11},{10,... | collective-permute-start | bytes 196616 | tf_op jit(solution)/shard_map/ppermute | solution.py:41
  87.8 4.5 %collective-permute-start.11 = (f32[1792,128]{1,0:T(8,128)S(1)}, f32[1792,128]{1,0:T(8,128)S(1)}, u32[]{:S(2)}, u32[]{:S(2)}) collective-permute-start(f32[1792,128]{1,0:T(8,128)S(1)} %shard_map.92), channel_id=1, source_target_pairs={{0,4},{4,0},{1,5},{5,1},{2,6},{6,2},{3,7},{7,3},{8,12},{12,8},{9,1... | collective-permute-start | bytes 2752520 | tf_op jit(solution)/shard_map/ppermute | solution.py:41
  130.3 5.6 %collective-permute-start.12 = (bf16[32,56,128]{2,1,0:T(8,128)(2,1)S(1)}, bf16[32,56,128]{2,1,0:T(8,128)(2,1)S(1)}, u32[]{:S(2)}, u32[]{:S(2)}) collective-permute-start(bf16[32,56,128]{2,1,0:T(8,128)(2,1)S(1)} %all_to_all.38.right), channel_id=1, source_target_pairs={{0,4},{4,0},{1,5},{5,1},{2,6},{6,2},{3,7},{7,3},{8,12},{12,8},{9,1... | collective-permute-start | bytes 1376264 | tf_op jit(solution)/shard_map/ppermute | solution.py:41
  137.2 6.0 %collective-permute-start.13 = (f32[128,256]{1,0:T(8,128)S(1)}, f32[128,256]{1,0:T(8,128)S(1)}, u32[]{:S(2)}, u32[]{:S(2)}) collective-permute-start(f32[128,256]{1,0:T(8,128)S(1)} %get-tuple-element.69), channel_id=1, source_target_pairs={{0,1},{1,2},{2,3},{3,0},{4,5},{5,6},{6,7},{7,4},{8,9},{9,10},{10,1... | collective-permute-start | bytes 393224 | tf_op jit(solution)/shard_map/ppermute | solution.py:41
  137.3 7.7 %collective-permute-start.14 = (f32[128,256]{1,0:T(8,128)S(1)}, f32[128,256]{1,0:T(8,128)S(1)}, u32[]{:S(2)}, u32[]{:S(2)}) collective-permute-start(f32[128,256]{1,0:T(8,128)S(1)} %get-tuple-element.70), channel_id=1, source_target_pairs={{0,3},{1,0},{2,1},{3,2},{4,7},{5,4},{6,5},{7,6},{8,11},{9,8},{10,9... | collective-permute-start | bytes 393224 | tf_op jit(solution)/shard_map/ppermute | solution.py:41
  140.0 5.6 %collective-permute-start.15 = (f32[128,256]{1,0:T(8,128)S(1)}, f32[128,256]{1,0:T(8,128)S(1)}, u32[]{:S(2)}, u32[]{:S(2)}) collective-permute-start(f32[128,256]{1,0:T(8,128)S(1)} %get-tuple-element.71), channel_id=1, source_target_pairs={{0,2},{1,3},{2,0},{3,1},{4,6},{5,7},{6,4},{7,5},{8,10},{9,11},{10,... | collective-permute-start | bytes 393224 | tf_op jit(solution)/shard_map/ppermute | solution.py:41
  145.8 6.2 %collective-permute-start.16 = (f32[128,256]{1,0:T(8,128)S(1)}, f32[128,256]{1,0:T(8,128)S(1)}, u32[]{:S(2)}, u32[]{:S(2)}) collective-permute-start(f32[128,256]{1,0:T(8,128)S(1)} %get-tuple-element.75.c0), channel_id=1, source_target_pairs={{0,3},{1,0},{2,1},{3,2},{4,7},{5,4},{6,5},{7,6},{8,11},{9,8},{10,9... | collective-permute-start | bytes 393224 | tf_op jit(solution)/shard_map/ppermute | solution.py:41
  148.9 5.4 %collective-permute-start.17 = (f32[128,256]{1,0:T(8,128)S(1)}, f32[128,256]{1,0:T(8,128)S(1)}, u32[]{:S(2)}, u32[]{:S(2)}) collective-permute-start(f32[128,256]{1,0:T(8,128)S(1)} %get-tuple-element.75.c0), channel_id=1, source_target_pairs={{0,2},{1,3},{2,0},{3,1},{4,6},{5,7},{6,4},{7,5},{8,10},{9,11},{10,... | collective-permute-start | bytes 393224 | tf_op jit(solution)/shard_map/ppermute | solution.py:41
  148.9 8.5 %collective-permute-start.18 = (f32[128,256]{1,0:T(8,128)S(1)}, f32[128,256]{1,0:T(8,128)S(1)}, u32[]{:S(2)}, u32[]{:S(2)}) collective-permute-start(f32[128,256]{1,0:T(8,128)S(1)} %get-tuple-element.75.c0), channel_id=1, source_target_pairs={{0,1},{1,2},{2,3},{3,0},{4,5},{5,6},{6,7},{7,4},{8,9},{9,10},{10,1... | collective-permute-start | bytes 393224 | tf_op jit(solution)/shard_map/ppermute | solution.py:41
  159.0 3.6 %collective-permute-start.19 = (f32[1792,128]{1,0:T(8,128)S(1)}, f32[1792,128]{1,0:T(8,128)S(1)}, u32[]{:S(2)}, u32[]{:S(2)}) collective-permute-start(f32[1792,128]{1,0:T(8,128)S(1)} %shard_map.100), channel_id=1, source_target_pairs={{0,4},{4,0},{1,5},{5,1},{2,6},{6,2},{3,7},{7,3},{8,12},{12,8},{9,1... | collective-permute-start | bytes 2752520 | tf_op jit(solution)/shard_map/ppermute | solution.py:41
  200.8 5.6 %collective-permute-start.20 = (bf16[32,56,128]{2,1,0:T(8,128)(2,1)S(1)}, bf16[32,56,128]{2,1,0:T(8,128)(2,1)S(1)}, u32[]{:S(2)}, u32[]{:S(2)}) collective-permute-start(bf16[32,56,128]{2,1,0:T(8,128)(2,1)S(1)} %all_to_all.40.right), channel_id=1, source_target_pairs={{0,4},{4,0},{1,5},{5,1},{2,6},{6,2},{3,7},{7,3},{8,12},{12,8},{9,1... | collective-permute-start | bytes 1376264 | tf_op jit(solution)/shard_map/ppermute | solution.py:41
  207.8 4.4 %collective-permute-start.21 = (bf16[128,256]{1,0:T(8,128)(2,1)S(1)}, bf16[128,256]{1,0:T(8,128)(2,1)S(1)}, u32[]{:S(2)}, u32[]{:S(2)}) collective-permute-start(bf16[128,256]{1,0:T(8,128)(2,1)S(1)} %get-tuple-element.79), channel_id=1, source_target_pairs={{0,1},{1,2},{2,3},{3,0},{4,5},{5,6},{6,7},{7,4},{8,9},{9,10},{10,1... | collective-permute-start | bytes 196616 | tf_op jit(solution)/shard_map/ppermute | solution.py:41
  207.9 4.7 %collective-permute-start.22 = (bf16[128,256]{1,0:T(8,128)(2,1)S(1)}, bf16[128,256]{1,0:T(8,128)(2,1)S(1)}, u32[]{:S(2)}, u32[]{:S(2)}) collective-permute-start(bf16[128,256]{1,0:T(8,128)(2,1)S(1)} %get-tuple-element.80), channel_id=1, source_target_pairs={{0,3},{1,0},{2,1},{3,2},{4,7},{5,4},{6,5},{7,6},{8,11},{9,8},{10,9... | collective-permute-start | bytes 196616 | tf_op jit(solution)/shard_map/ppermute | solution.py:41
  210.6 4.6 %collective-permute-start.23 = (bf16[128,256]{1,0:T(8,128)(2,1)S(1)}, bf16[128,256]{1,0:T(8,128)(2,1)S(1)}, u32[]{:S(2)}, u32[]{:S(2)}) collective-permute-start(bf16[128,256]{1,0:T(8,128)(2,1)S(1)} %get-tuple-element.81), channel_id=1, source_target_pairs={{0,2},{1,3},{2,0},{3,1},{4,6},{5,7},{6,4},{7,5},{8,10},{9,11},{10,... | collective-permute-start | bytes 196616 | tf_op jit(solution)/shard_map/ppermute | solution.py:41
  216.0 20.7 %all-to-all-start.6 = ((f32[256,1,128]{2,1,0:T(1,128)}), f32[256,1,128]{2,1,0:T(1,128)S(1)}, u32[]{:S(2)}, u32[]{:S(2)}) async-start(f32[256,1,128]{2,1,0:T(1,128)} %bitcast.1), calls=%async_computation.6 | async-start | bytes 262144 | tf_op jit(solution)/shard_map/all_to_all | solution.py:468
  224.0 4.8 %collective-permute-start.24 = (f32[8,256]{1,0:T(8,128)S(1)}, f32[8,256]{1,0:T(8,128)S(1)}, u32[]{:S(2)}, u32[]{:S(2)}) collective-permute-start(f32[8,256]{1,0:T(8,128)S(1)} %get-tuple-element.88.n0), channel_id=1, source_target_pairs={{0,3},{1,0},{2,1},{3,2},{4,7},{5,4},{6,5},{7,6},{8,11},{9,8},{10,9... | collective-permute-start | bytes 24584 | tf_op jit(solution)/shard_map/ppermute | solution.py:41
  226.6 4.3 %collective-permute-start.25 = (f32[8,256]{1,0:T(8,128)S(1)}, f32[8,256]{1,0:T(8,128)S(1)}, u32[]{:S(2)}, u32[]{:S(2)}) collective-permute-start(f32[8,256]{1,0:T(8,128)S(1)} %get-tuple-element.88.n0), channel_id=1, source_target_pairs={{0,2},{1,3},{2,0},{3,1},{4,6},{5,7},{6,4},{7,5},{8,10},{9,11},{10,... | collective-permute-start | bytes 24584 | tf_op jit(solution)/shard_map/ppermute | solution.py:41
  227.2 4.0 %collective-permute-start.26 = (f32[8,256]{1,0:T(8,128)S(1)}, f32[8,256]{1,0:T(8,128)S(1)}, u32[]{:S(2)}, u32[]{:S(2)}) collective-permute-start(f32[8,256]{1,0:T(8,128)S(1)} %get-tuple-element.88.n0), channel_id=1, source_target_pairs={{0,1},{1,2},{2,3},{3,0},{4,5},{5,6},{6,7},{7,4},{8,9},{9,10},{10,1... | collective-permute-start | bytes 24584 | tf_op jit(solution)/shard_map/ppermute | solution.py:41

commit v3 on v2

--- a/solution.py
+++ b/solution.py
@@ -344,17 +344,21 @@
 
 
 def last_norms(parts, current, stats, n0, n1, at, devices):
-    def body(own, r1, r2, r3, current, stats, n0, n1, norms_out, copies):
+    tasks, width = current.shape
+
+    def body(own, r1, r2, r3, current, stats, n0, n1, packed, copies):
         gradient = own[...]
         for share in (r1, r2, r3):
             gradient += share[...].astype(F32)
         norms = lane_norms(gradient)
-        norms_out[...] = jnp.concatenate([n0[...], n1[...], norms] + [norms] * 5, axis=0)
+        out_rows = jnp.concatenate([n0[...], n1[...], norms] + [norms] * 5, axis=0)
+        packed[:tasks, :] = current[...]
+        packed[tasks:, :] = out_rows
         row = lane(stats[...], at + 2, jnp.sum(lane_norms(current[...])))
         row = lane(row, at + 3, jnp.max(norms))
         copies[...] = jnp.broadcast_to(row, copies.shape)
 
-    outs = [shape_of((8, n0.shape[1])), shape_of((devices, stats.shape[1]))]
+    outs = [shape_of((tasks + 8, width)), shape_of((devices, stats.shape[1]))]
     return call(body, outs, *parts, current, stats, n0, n1)
 
 
@@ -384,7 +388,8 @@
             wide = jnp.concatenate([scale] * (width // 128), axis=1)
             for k, block in enumerate((n0, n1, n2, n3)):
                 start = block_at(k, width)
-                correlations[t : t + 1, pl.ds(start, width)] = block[t : t + 1, :] / wide
+                row_at = block.shape[0] - 8 + t
+                correlations[t : t + 1, pl.ds(start, width)] = block[row_at : row_at + 1, :] / wide
         for t in range(ITERS + 1):
             gaps[t] = jnp.sum(jnp.where(at_lane == t, row, 0.0))
         for t in range(ITERS):
@@ -395,11 +400,11 @@
 
 
 def turned_back(blocks):
-    tasks, width = blocks[0].shape
+    tasks, width = blocks[0].shape[0] - 8, blocks[0].shape[1]
 
     def body(c0, c1, c2, c3, out):
         for k, block in enumerate((c0, c1, c2, c3)):
-            out[pl.ds(block_at(k, width), width), :] = block[...].T
+            out[pl.ds(block_at(k, width), width), :] = block[:tasks, :].T
 
     return call(body, shape_of((4 * width, tasks)), *blocks)
 
@@ -456,15 +461,14 @@
         if t < ITERS:
             current, sent, own_norms, stats, tops = prox(
                 shares, current, steps, active_mask, penalty_index, stats, 8 * t,
-                BF if t + 1 < ITERS else F32, tops,
+                BF, tops,
             )
             norms.append(own_norms)
             blocks = from_owners(sent)
-            if t + 1 == ITERS:
-                coefficients = turned_back(blocks)
         else:
             packed, copies = last_norms(shares, current, stats, *norms, 8 * t, devices)
     norm_blocks = from_owners(packed)
+    coefficients = turned_back(norm_blocks)
     everyone = lax.all_to_all(copies[:, None, :], ALL, split_axis=0, concat_axis=0, tiled=True)
     correlations, gaps, counts = finish(
         everyone.reshape(copies.shape), tops, penalty_index, norm_blocks

time: 238 us -> 235 us (0.987)
  waiting for transfers between devices: 37.7 us -> 32.5 us
  starting transfers between devices: 54.7 us -> 57.2 us
    all_to_all x1, waiting for transfers between devices: 5.52 us -> 0.35 us  [local(): lax.all_to_all(copies[:, None, :], ALL, split_axis=0, concat_axis=0, tile...]
    ppermute x27, starting transfers between devices: 46.8 us -> 49.2 us  [shifted(): return lax.ppermute(value, axis, [(i, (i + by) % n) for i in range(n)])]
  transfers between devices with their start and end apart: 28 -> 28, of which waited for: 25 -> 26; matrix products, arithmetic and copies ran while one was open for 0% -> 0% of each run, Pallas kernels for 4% -> 4%
where the time goes in v3:
time: 235 us
  blocking collectives  116 us (49%)
  starting transfers between devices  57.2 us (24%)
  waiting for transfers between devices  32.5 us (14%)
  Pallas kernels  27.7 us (12%)
    all_to_all x6, blocking collectives, plane_exchange(): lax.all_to_all(blocks, PLANE, split_axis=0, concat_axis=0, tiled=True)  116 us
    ppermute x27, starting transfers between devices, shifted(): return lax.ppermute(value, axis, [(i, (i + by) % n) for i in range(n)])  49.2 us
    ppermute x27, waiting for transfers between devices, shifted(): return lax.ppermute(value, axis, [(i, (i + by) % n) for i in range(n)])  32.2 us
    pallas_call x23, Pallas kernels, call(): pl.pallas_call(body, out_shape=shapes[0] if single else tuple(shapes), in...  22.4 us
    all_to_all x1, starting transfers between devices, local(): lax.all_to_all(copies[:, None, :], ALL, split_axis=0, concat_axis=0, tile...  7.92 us
    pallas_call x1, Pallas kernels, corr_first(): pl.pallas_call(body, out_shape=(shape_of((tasks + 2 * EXTRA, width)), *[s...  5.3 us
  transfers between devices with their start and end apart: 28, of which 26 were waited for; matrix products, arithmetic and copies ran while one was open for 0% of the time, Pallas kernels for 4%

profile of v3, /device:TPU:1, one launch (start us, length us, event | category | flops | bytes accessed | tf_op | source)
XLA Modules:
  0.0 235.0 jit_solution(12554805845283423250)
XLA Ops:
  0.6 5.3 %corr_first.1 = (f32[144,256]{1,0:T(8,128)S(1)}, bf16[144,256]{1,0:T(8,128)(2,1)S(1)}, bf16[144,256]{1,0:T(8,128)(2,1)S(1)}, bf16[144,256]{1,0:T(8,128)(2,1)S(1)...) custom-call(bf16[3584,1024]{1,0:T(8,128)(2,1)} %design.1, bf16[3584,128]{1,0:T(8,128)(2,1)} %targets.1), custom_call_target="tpu_custom_call" | custom-call | tf_op jit(solution)/shard_map/corr_first/pallas_call | solution.py:125
  6.0 1.7 shard_map.85
  7.6 3.3 %collective-permute-start = (f32[1792,128]{1,0:T(8,128)S(1)}, f32[1792,128]{1,0:T(8,128)S(1)}, u32[]{:S(2)}, u32[]{:S(2)}) collective-permute-start(f32[1792,128]{1,0:T(8,128)S(1)} %shard_map.85), channel_id=1, source_target_pairs={{0,4},{4,0},{1,5},{5,1},{2,6},{6,2},{3,7},{7,3},{8,12},{12,8},{9,1... | collective-permute-start | bytes 2752520 | tf_op jit(solution)/shard_map/ppermute | solution.py:41
  10.9 2.7 %collective-permute-start.2 = (bf16[144,256]{1,0:T(8,128)(2,1)S(1)}, bf16[144,256]{1,0:T(8,128)(2,1)S(1)}, u32[]{:S(2)}, u32[]{:S(2)}) collective-permute-start(bf16[144,256]{1,0:T(8,128)(2,1)S(1)} %get-tuple-element.52), channel_id=1, source_target_pairs={{0,3},{1,0},{2,1},{3,2},{4,7},{5,4},{6,5},{7,6},{8,11},{9,8},{10,9... | collective-permute-start | bytes 221192 | tf_op jit(solution)/shard_map/ppermute | solution.py:41
  13.6 1.8 shard_map.84
  18.6 21.1 %all_to_all.35.parts = bf16[32,56,128]{2,1,0:T(8,128)(2,1)S(1)} all-to-all(bf16[32,56,128]{2,1,0:T(8,128)(2,1)S(1)} %get-tuple-element.54), channel_id=1, replica_groups=mesh['y'=4,'z'=8,'core'=2,'samp'=4] {'y','z'}, dimensions={0} | all-to-all | bytes 917504 | tf_op jit(solution)/shard_map/all_to_all | solution.py:422
  39.9 19.2 %all_to_all.36.right.refs_0_ = bf16[32,64,128]{2,1,0:T(8,128)(2,1)S(1)} all-to-all(bf16[32,64,128]{2,1,0:T(8,128)(2,1)S(1)} %get-tuple-element.57), channel_id=1, replica_groups=mesh['y'=4,'z'=8,'core'=2,'samp'=4] {'y','z'}, dimensions={0} | all-to-all | bytes 1048576 | tf_op jit(solution)/shard_map/all_to_all | solution.py:422
  59.1 5.4 %collective-permute-start.4 = (bf16[32,64,128]{2,1,0:T(8,128)(2,1)S(1)}, bf16[32,64,128]{2,1,0:T(8,128)(2,1)S(1)}, u32[]{:S(2)}, u32[]{:S(2)}) collective-permute-start(bf16[32,64,128]{2,1,0:T(8,128)(2,1)S(1)} %all_to_all.36.right.refs_0_), channel_id=1, source_target_pairs={{0,4},{4,0},{1,5},{5,1},{2,6},{6,2},{3,7},{7,3},{8,12},{12,8},{9,1... | collective-permute-start | bytes 1572872 | tf_op jit(solution)/shard_map/ppermute | solution.py:41
  67.6 2.9 %collective-permute-start.5 = (f32[136,256]{1,0:T(8,128)S(1)}, f32[136,256]{1,0:T(8,128)S(1)}, u32[]{:S(2)}, u32[]{:S(2)}) collective-permute-start(f32[136,256]{1,0:T(8,128)S(1)} %get-tuple-element.59), channel_id=1, source_target_pairs={{0,1},{1,2},{2,3},{3,0},{4,5},{5,6},{6,7},{7,4},{8,9},{9,10},{10,1... | collective-permute-start | bytes 417800 | tf_op jit(solution)/shard_map/ppermute | solution.py:41
  70.6 1.9 collective-permute-start.7
  78.2 3.8 %collective-permute-start.9 = (bf16[128,256]{1,0:T(8,128)(2,1)S(1)}, bf16[128,256]{1,0:T(8,128)(2,1)S(1)}, u32[]{:S(2)}, u32[]{:S(2)}) collective-permute-start(bf16[128,256]{1,0:T(8,128)(2,1)S(1)} %get-tuple-element.65.c0), channel_id=1, source_target_pairs={{0,2},{1,3},{2,0},{3,1},{4,6},{5,7},{6,4},{7,5},{8,10},{9,11},{10,... | collective-permute-start | bytes 196616 | tf_op jit(solution)/shard_map/ppermute | solution.py:41
  82.4 2.0 collective-permute-done.9.c2
  84.4 1.7 collective-permute-done.8.c1
  87.7 2.3 collective-permute-start.11
  90.0 1.6 shard_map.91.near
  92.2 18.0 %all_to_all.37.parts = bf16[32,56,128]{2,1,0:T(8,128)(2,1)S(1)} all-to-all(bf16[32,56,128]{2,1,0:T(8,128)(2,1)S(1)} %shard_map.93), channel_id=1, replica_groups=mesh['y'=4,'z'=8,'core'=2,'samp'=4] {'y','z'}, dimensions={0} | all-to-all | bytes 917504 | tf_op jit(solution)/shard_map/all_to_all | solution.py:422
  110.4 19.7 %all_to_all.38.right = bf16[32,56,128]{2,1,0:T(8,128)(2,1)S(1)} all-to-all(bf16[32,56,128]{2,1,0:T(8,128)(2,1)S(1)} %get-tuple-element.67), channel_id=1, replica_groups=mesh['y'=4,'z'=8,'core'=2,'samp'=4] {'y','z'}, dimensions={0} | all-to-all | bytes 917504 | tf_op jit(solution)/shard_map/all_to_all | solution.py:422
  130.1 4.1 %collective-permute-start.12 = (bf16[32,56,128]{2,1,0:T(8,128)(2,1)S(1)}, bf16[32,56,128]{2,1,0:T(8,128)(2,1)S(1)}, u32[]{:S(2)}, u32[]{:S(2)}) collective-permute-start(bf16[32,56,128]{2,1,0:T(8,128)(2,1)S(1)} %all_to_all.38.right), channel_id=1, source_target_pairs={{0,4},{4,0},{1,5},{5,1},{2,6},{6,2},{3,7},{7,3},{8,12},{12,8},{9,1... | collective-permute-start | bytes 1376264 | tf_op jit(solution)/shard_map/ppermute | solution.py:41
  137.2 2.7 %collective-permute-start.14 = (f32[128,256]{1,0:T(8,128)S(1)}, f32[128,256]{1,0:T(8,128)S(1)}, u32[]{:S(2)}, u32[]{:S(2)}) collective-permute-start(f32[128,256]{1,0:T(8,128)S(1)} %get-tuple-element.70), channel_id=1, source_target_pairs={{0,3},{1,0},{2,1},{3,2},{4,7},{5,4},{6,5},{7,6},{8,11},{9,8},{10,9... | collective-permute-start | bytes 393224 | tf_op jit(solution)/shard_map/ppermute | solution.py:41
  139.9 3.2 %collective-permute-done.13.r1 = f32[128,256]{1,0:T(8,128)S(1)} collective-permute-done((f32[128,256]{1,0:T(8,128)S(1)}, f32[128,256]{1,0:T(8,128)S(1)}, u32[]{:S(2)}, u32[]{:S(2)}) %collective-permute-start.13) | collective-permute-done | bytes 131104 | tf_op jit(solution)/shard_map/ppermute | solution.py:41
  143.1 1.9 collective-permute-done.14.r2
  146.5 3.5 %collective-permute-start.17 = (bf16[128,256]{1,0:T(8,128)(2,1)S(1)}, bf16[128,256]{1,0:T(8,128)(2,1)S(1)}, u32[]{:S(2)}, u32[]{:S(2)}) collective-permute-start(bf16[128,256]{1,0:T(8,128)(2,1)S(1)} %get-tuple-element.75.c0), channel_id=1, source_target_pairs={{0,2},{1,3},{2,0},{3,1},{4,6},{5,7},{6,4},{7,5},{8,10},{9,11},{10,... | collective-permute-start | bytes 196616 | tf_op jit(solution)/shard_map/ppermute | solution.py:41
  150.5 2.0 collective-permute-done.17.c2
  155.7 2.1 collective-permute-start.19
  160.0 18.2 %all_to_all.39.parts = bf16[32,56,128]{2,1,0:T(8,128)(2,1)S(1)} all-to-all(bf16[32,56,128]{2,1,0:T(8,128)(2,1)S(1)} %shard_map.100), channel_id=1, replica_groups=mesh['y'=4,'z'=8,'core'=2,'samp'=4] {'y','z'}, dimensions={0} | all-to-all | bytes 917504 | tf_op jit(solution)/shard_map/all_to_all | solution.py:422
  178.4 19.7 %all_to_all.40.right = bf16[32,56,128]{2,1,0:T(8,128)(2,1)S(1)} all-to-all(bf16[32,56,128]{2,1,0:T(8,128)(2,1)S(1)} %get-tuple-element.77), channel_id=1, replica_groups=mesh['y'=4,'z'=8,'core'=2,'samp'=4] {'y','z'}, dimensions={0} | all-to-all | bytes 917504 | tf_op jit(solution)/shard_map/all_to_all | solution.py:422
  198.1 4.1 %collective-permute-start.20 = (bf16[32,56,128]{2,1,0:T(8,128)(2,1)S(1)}, bf16[32,56,128]{2,1,0:T(8,128)(2,1)S(1)}, u32[]{:S(2)}, u32[]{:S(2)}) collective-permute-start(bf16[32,56,128]{2,1,0:T(8,128)(2,1)S(1)} %all_to_all.40.right), channel_id=1, source_target_pairs={{0,4},{4,0},{1,5},{5,1},{2,6},{6,2},{3,7},{7,3},{8,12},{12,8},{9,1... | collective-permute-start | bytes 1376264 | tf_op jit(solution)/shard_map/ppermute | solution.py:41
  205.2 2.7 %collective-permute-start.22 = (bf16[128,256]{1,0:T(8,128)(2,1)S(1)}, bf16[128,256]{1,0:T(8,128)(2,1)S(1)}, u32[]{:S(2)}, u32[]{:S(2)}) collective-permute-start(bf16[128,256]{1,0:T(8,128)(2,1)S(1)} %get-tuple-element.80), channel_id=1, source_target_pairs={{0,3},{1,0},{2,1},{3,2},{4,7},{5,4},{6,5},{7,6},{8,11},{9,8},{10,9... | collective-permute-start | bytes 196616 | tf_op jit(solution)/shard_map/ppermute | solution.py:41
  209.8 2.6 %collective-permute-done.23.r3 = bf16[128,256]{1,0:T(8,128)(2,1)S(1)} collective-permute-done((bf16[128,256]{1,0:T(8,128)(2,1)S(1)}, bf16[128,256]{1,0:T(8,128)(2,1)S(1)}, u32[]{:S(2)}, u32[]{:S(2)}) %collective-permute-start.23) | collective-permute-done | bytes 65568 | tf_op jit(solution)/shard_map/ppermute | solution.py:41
  213.3 7.9 %all-to-all-start.6 = ((f32[256,1,128]{2,1,0:T(1,128)}), f32[256,1,128]{2,1,0:T(1,128)S(1)}, u32[]{:S(2)}, u32[]{:S(2)}) async-start(f32[256,1,128]{2,1,0:T(1,128)} %bitcast.1), calls=%async_computation.6 | async-start | bytes 262144 | tf_op jit(solution)/shard_map/all_to_all | solution.py:472
  222.6 2.4 %collective-permute-start.25 = (f32[136,256]{1,0:T(8,128)S(1)}, f32[136,256]{1,0:T(8,128)S(1)}, u32[]{:S(2)}, u32[]{:S(2)}) collective-permute-start(f32[136,256]{1,0:T(8,128)S(1)} %get-tuple-element.86.c0.n0), channel_id=1, source_target_pairs={{0,2},{1,3},{2,0},{3,1},{4,6},{5,7},{6,4},{7,5},{8,10},{9,11},{10,... | collective-permute-start | bytes 417800 | tf_op jit(solution)/shard_map/ppermute | solution.py:41
  227.0 5.7 %collective-permute-done.25.c2.n2 = f32[136,256]{1,0:T(8,128)S(1)} collective-permute-done((f32[136,256]{1,0:T(8,128)S(1)}, f32[136,256]{1,0:T(8,128)S(1)}, u32[]{:S(2)}, u32[]{:S(2)}) %collective-permute-start.25) | collective-permute-done | bytes 139296 | tf_op jit(solution)/shard_map/ppermute | solution.py:41
  (58 shorter events, 36.2 us)
Async XLA Ops:
  0.6 5.3 %copy-start = (f32[1024,128]{1,0:T(8,128)S(1)}, f32[1024,128]{1,0:T(8,128)}, u32[]{:S(2)}) copy-start(f32[1024,128]{1,0:T(8,128)} %warm.3) | copy-start | bytes 1572868
  7.6 10.7 %collective-permute-start = (f32[1792,128]{1,0:T(8,128)S(1)}, f32[1792,128]{1,0:T(8,128)S(1)}, u32[]{:S(2)}, u32[]{:S(2)}) collective-permute-start(f32[1792,128]{1,0:T(8,128)S(1)} %shard_map.85), channel_id=1, source_target_pairs={{0,4},{4,0},{1,5},{5,1},{2,6},{6,2},{3,7},{7,3},{8,12},{12,8},{9,1... | collective-permute-start | bytes 2752520 | tf_op jit(solution)/shard_map/ppermute | solution.py:41
  10.9 4.9 %collective-permute-start.1 = (bf16[144,256]{1,0:T(8,128)(2,1)S(1)}, bf16[144,256]{1,0:T(8,128)(2,1)S(1)}, u32[]{:S(2)}, u32[]{:S(2)}) collective-permute-start(bf16[144,256]{1,0:T(8,128)(2,1)S(1)} %get-tuple-element.51), channel_id=1, source_target_pairs={{0,1},{1,2},{2,3},{3,0},{4,5},{5,6},{6,7},{7,4},{8,9},{9,10},{10,1... | collective-permute-start | bytes 221192 | tf_op jit(solution)/shard_map/ppermute | solution.py:41
  10.9 5.8 %collective-permute-start.2 = (bf16[144,256]{1,0:T(8,128)(2,1)S(1)}, bf16[144,256]{1,0:T(8,128)(2,1)S(1)}, u32[]{:S(2)}, u32[]{:S(2)}) collective-permute-start(bf16[144,256]{1,0:T(8,128)(2,1)S(1)} %get-tuple-element.52), channel_id=1, source_target_pairs={{0,3},{1,0},{2,1},{3,2},{4,7},{5,4},{6,5},{7,6},{8,11},{9,8},{10,9... | collective-permute-start | bytes 221192 | tf_op jit(solution)/shard_map/ppermute | solution.py:41
  13.6 4.7 %collective-permute-start.3 = (bf16[144,256]{1,0:T(8,128)(2,1)S(1)}, bf16[144,256]{1,0:T(8,128)(2,1)S(1)}, u32[]{:S(2)}, u32[]{:S(2)}) collective-permute-start(bf16[144,256]{1,0:T(8,128)(2,1)S(1)} %get-tuple-element.53), channel_id=1, source_target_pairs={{0,2},{1,3},{2,0},{3,1},{4,6},{5,7},{6,4},{7,5},{8,10},{9,11},{10,... | collective-permute-start | bytes 221192 | tf_op jit(solution)/shard_map/ppermute | solution.py:41
  59.1 17.4 %copy-start.1 = (s32[2,1024]{1,0:T(2,128)S(1)}, s32[2,1024]{1,0:T(2,128)}, u32[]{:S(2)}) copy-start(s32[2,1024]{1,0:T(2,128)} %mask.3) | copy-start | bytes 24580
  59.1 6.9 %collective-permute-start.4 = (bf16[32,64,128]{2,1,0:T(8,128)(2,1)S(1)}, bf16[32,64,128]{2,1,0:T(8,128)(2,1)S(1)}, u32[]{:S(2)}, u32[]{:S(2)}) collective-permute-start(bf16[32,64,128]{2,1,0:T(8,128)(2,1)S(1)} %all_to_all.36.right.refs_0_), channel_id=1, source_target_pairs={{0,4},{4,0},{1,5},{5,1},{2,6},{6,2},{3,7},{7,3},{8,12},{12,8},{9,1... | collective-permute-start | bytes 1572872 | tf_op jit(solution)/shard_map/ppermute | solution.py:41
  67.6 6.1 %collective-permute-start.5 = (f32[136,256]{1,0:T(8,128)S(1)}, f32[136,256]{1,0:T(8,128)S(1)}, u32[]{:S(2)}, u32[]{:S(2)}) collective-permute-start(f32[136,256]{1,0:T(8,128)S(1)} %get-tuple-element.59), channel_id=1, source_target_pairs={{0,1},{1,2},{2,3},{3,0},{4,5},{5,6},{6,7},{7,4},{8,9},{9,10},{10,1... | collective-permute-start | bytes 417800 | tf_op jit(solution)/shard_map/ppermute | solution.py:41
  70.5 4.6 %collective-permute-start.6 = (f32[136,256]{1,0:T(8,128)S(1)}, f32[136,256]{1,0:T(8,128)S(1)}, u32[]{:S(2)}, u32[]{:S(2)}) collective-permute-start(f32[136,256]{1,0:T(8,128)S(1)} %get-tuple-element.60), channel_id=1, source_target_pairs={{0,3},{1,0},{2,1},{3,2},{4,7},{5,4},{6,5},{7,6},{8,11},{9,8},{10,9... | collective-permute-start | bytes 417800 | tf_op jit(solution)/shard_map/ppermute | solution.py:41
  70.6 6.0 %collective-permute-start.7 = (f32[136,256]{1,0:T(8,128)S(1)}, f32[136,256]{1,0:T(8,128)S(1)}, u32[]{:S(2)}, u32[]{:S(2)}) collective-permute-start(f32[136,256]{1,0:T(8,128)S(1)} %get-tuple-element.61), channel_id=1, source_target_pairs={{0,2},{1,3},{2,0},{3,1},{4,6},{5,7},{6,4},{7,5},{8,10},{9,11},{10,... | collective-permute-start | bytes 417800 | tf_op jit(solution)/shard_map/ppermute | solution.py:41
  76.7 5.7 %collective-permute-start.10 = (bf16[128,256]{1,0:T(8,128)(2,1)S(1)}, bf16[128,256]{1,0:T(8,128)(2,1)S(1)}, u32[]{:S(2)}, u32[]{:S(2)}) collective-permute-start(bf16[128,256]{1,0:T(8,128)(2,1)S(1)} %get-tuple-element.65.c0), channel_id=1, source_target_pairs={{0,1},{1,2},{2,3},{3,0},{4,5},{5,6},{6,7},{7,4},{8,9},{9,10},{10,1... | collective-permute-start | bytes 196616 | tf_op jit(solution)/shard_map/ppermute | solution.py:41
  78.2 6.2 %collective-permute-start.9 = (bf16[128,256]{1,0:T(8,128)(2,1)S(1)}, bf16[128,256]{1,0:T(8,128)(2,1)S(1)}, u32[]{:S(2)}, u32[]{:S(2)}) collective-permute-start(bf16[128,256]{1,0:T(8,128)(2,1)S(1)} %get-tuple-element.65.c0), channel_id=1, source_target_pairs={{0,2},{1,3},{2,0},{3,1},{4,6},{5,7},{6,4},{7,5},{8,10},{9,11},{10,... | collective-permute-start | bytes 196616 | tf_op jit(solution)/shard_map/ppermute | solution.py:41
  82.0 4.1 %collective-permute-start.8 = (bf16[128,256]{1,0:T(8,128)(2,1)S(1)}, bf16[128,256]{1,0:T(8,128)(2,1)S(1)}, u32[]{:S(2)}, u32[]{:S(2)}) collective-permute-start(bf16[128,256]{1,0:T(8,128)(2,1)S(1)} %get-tuple-element.65.c0), channel_id=1, source_target_pairs={{0,3},{1,0},{2,1},{3,2},{4,7},{5,4},{6,5},{7,6},{8,11},{9,8},{10,9... | collective-permute-start | bytes 196616 | tf_op jit(solution)/shard_map/ppermute | solution.py:41
  87.7 4.4 %collective-permute-start.11 = (f32[1792,128]{1,0:T(8,128)S(1)}, f32[1792,128]{1,0:T(8,128)S(1)}, u32[]{:S(2)}, u32[]{:S(2)}) collective-permute-start(f32[1792,128]{1,0:T(8,128)S(1)} %shard_map.92), channel_id=1, source_target_pairs={{0,4},{4,0},{1,5},{5,1},{2,6},{6,2},{3,7},{7,3},{8,12},{12,8},{9,1... | collective-permute-start | bytes 2752520 | tf_op jit(solution)/shard_map/ppermute | solution.py:41
  130.1 5.6 %collective-permute-start.12 = (bf16[32,56,128]{2,1,0:T(8,128)(2,1)S(1)}, bf16[32,56,128]{2,1,0:T(8,128)(2,1)S(1)}, u32[]{:S(2)}, u32[]{:S(2)}) collective-permute-start(bf16[32,56,128]{2,1,0:T(8,128)(2,1)S(1)} %all_to_all.38.right), channel_id=1, source_target_pairs={{0,4},{4,0},{1,5},{5,1},{2,6},{6,2},{3,7},{7,3},{8,12},{12,8},{9,1... | collective-permute-start | bytes 1376264 | tf_op jit(solution)/shard_map/ppermute | solution.py:41
  137.1 6.0 %collective-permute-start.13 = (f32[128,256]{1,0:T(8,128)S(1)}, f32[128,256]{1,0:T(8,128)S(1)}, u32[]{:S(2)}, u32[]{:S(2)}) collective-permute-start(f32[128,256]{1,0:T(8,128)S(1)} %get-tuple-element.69), channel_id=1, source_target_pairs={{0,1},{1,2},{2,3},{3,0},{4,5},{5,6},{6,7},{7,4},{8,9},{9,10},{10,1... | collective-permute-start | bytes 393224 | tf_op jit(solution)/shard_map/ppermute | solution.py:41
  137.2 7.8 %collective-permute-start.14 = (f32[128,256]{1,0:T(8,128)S(1)}, f32[128,256]{1,0:T(8,128)S(1)}, u32[]{:S(2)}, u32[]{:S(2)}) collective-permute-start(f32[128,256]{1,0:T(8,128)S(1)} %get-tuple-element.70), channel_id=1, source_target_pairs={{0,3},{1,0},{2,1},{3,2},{4,7},{5,4},{6,5},{7,6},{8,11},{9,8},{10,9... | collective-permute-start | bytes 393224 | tf_op jit(solution)/shard_map/ppermute | solution.py:41
  139.8 5.6 %collective-permute-start.15 = (f32[128,256]{1,0:T(8,128)S(1)}, f32[128,256]{1,0:T(8,128)S(1)}, u32[]{:S(2)}, u32[]{:S(2)}) collective-permute-start(f32[128,256]{1,0:T(8,128)S(1)} %get-tuple-element.71), channel_id=1, source_target_pairs={{0,2},{1,3},{2,0},{3,1},{4,6},{5,7},{6,4},{7,5},{8,10},{9,11},{10,... | collective-permute-start | bytes 393224 | tf_op jit(solution)/shard_map/ppermute | solution.py:41
  145.7 4.8 %collective-permute-start.18 = (bf16[128,256]{1,0:T(8,128)(2,1)S(1)}, bf16[128,256]{1,0:T(8,128)(2,1)S(1)}, u32[]{:S(2)}, u32[]{:S(2)}) collective-permute-start(bf16[128,256]{1,0:T(8,128)(2,1)S(1)} %get-tuple-element.75.c0), channel_id=1, source_target_pairs={{0,1},{1,2},{2,3},{3,0},{4,5},{5,6},{6,7},{7,4},{8,9},{9,10},{10,1... | collective-permute-start | bytes 196616 | tf_op jit(solution)/shard_map/ppermute | solution.py:41
  146.5 6.0 %collective-permute-start.17 = (bf16[128,256]{1,0:T(8,128)(2,1)S(1)}, bf16[128,256]{1,0:T(8,128)(2,1)S(1)}, u32[]{:S(2)}, u32[]{:S(2)}) collective-permute-start(bf16[128,256]{1,0:T(8,128)(2,1)S(1)} %get-tuple-element.75.c0), channel_id=1, source_target_pairs={{0,2},{1,3},{2,0},{3,1},{4,6},{5,7},{6,4},{7,5},{8,10},{9,11},{10,... | collective-permute-start | bytes 196616 | tf_op jit(solution)/shard_map/ppermute | solution.py:41
  150.0 4.0 %collective-permute-start.16 = (bf16[128,256]{1,0:T(8,128)(2,1)S(1)}, bf16[128,256]{1,0:T(8,128)(2,1)S(1)}, u32[]{:S(2)}, u32[]{:S(2)}) collective-permute-start(bf16[128,256]{1,0:T(8,128)(2,1)S(1)} %get-tuple-element.75.c0), channel_id=1, source_target_pairs={{0,3},{1,0},{2,1},{3,2},{4,7},{5,4},{6,5},{7,6},{8,11},{9,8},{10,9... | collective-permute-start | bytes 196616 | tf_op jit(solution)/shard_map/ppermute | solution.py:41
  155.7 4.2 %collective-permute-start.19 = (f32[1792,128]{1,0:T(8,128)S(1)}, f32[1792,128]{1,0:T(8,128)S(1)}, u32[]{:S(2)}, u32[]{:S(2)}) collective-permute-start(f32[1792,128]{1,0:T(8,128)S(1)} %shard_map.99), channel_id=1, source_target_pairs={{0,4},{4,0},{1,5},{5,1},{2,6},{6,2},{3,7},{7,3},{8,12},{12,8},{9,1... | collective-permute-start | bytes 2752520 | tf_op jit(solution)/shard_map/ppermute | solution.py:41
  198.1 5.6 %collective-permute-start.20 = (bf16[32,56,128]{2,1,0:T(8,128)(2,1)S(1)}, bf16[32,56,128]{2,1,0:T(8,128)(2,1)S(1)}, u32[]{:S(2)}, u32[]{:S(2)}) collective-permute-start(bf16[32,56,128]{2,1,0:T(8,128)(2,1)S(1)} %all_to_all.40.right), channel_id=1, source_target_pairs={{0,4},{4,0},{1,5},{5,1},{2,6},{6,2},{3,7},{7,3},{8,12},{12,8},{9,1... | collective-permute-start | bytes 1376264 | tf_op jit(solution)/shard_map/ppermute | solution.py:41
  205.1 4.4 %collective-permute-start.21 = (bf16[128,256]{1,0:T(8,128)(2,1)S(1)}, bf16[128,256]{1,0:T(8,128)(2,1)S(1)}, u32[]{:S(2)}, u32[]{:S(2)}) collective-permute-start(bf16[128,256]{1,0:T(8,128)(2,1)S(1)} %get-tuple-element.79), channel_id=1, source_target_pairs={{0,1},{1,2},{2,3},{3,0},{4,5},{5,6},{6,7},{7,4},{8,9},{9,10},{10,1... | collective-permute-start | bytes 196616 | tf_op jit(solution)/shard_map/ppermute | solution.py:41
  205.2 4.7 %collective-permute-start.22 = (bf16[128,256]{1,0:T(8,128)(2,1)S(1)}, bf16[128,256]{1,0:T(8,128)(2,1)S(1)}, u32[]{:S(2)}, u32[]{:S(2)}) collective-permute-start(bf16[128,256]{1,0:T(8,128)(2,1)S(1)} %get-tuple-element.80), channel_id=1, source_target_pairs={{0,3},{1,0},{2,1},{3,2},{4,7},{5,4},{6,5},{7,6},{8,11},{9,8},{10,9... | collective-permute-start | bytes 196616 | tf_op jit(solution)/shard_map/ppermute | solution.py:41
  207.8 4.6 %collective-permute-start.23 = (bf16[128,256]{1,0:T(8,128)(2,1)S(1)}, bf16[128,256]{1,0:T(8,128)(2,1)S(1)}, u32[]{:S(2)}, u32[]{:S(2)}) collective-permute-start(bf16[128,256]{1,0:T(8,128)(2,1)S(1)} %get-tuple-element.81), channel_id=1, source_target_pairs={{0,2},{1,3},{2,0},{3,1},{4,6},{5,7},{6,4},{7,5},{8,10},{9,11},{10,... | collective-permute-start | bytes 196616 | tf_op jit(solution)/shard_map/ppermute | solution.py:41
  213.3 20.7 %all-to-all-start.6 = ((f32[256,1,128]{2,1,0:T(1,128)}), f32[256,1,128]{2,1,0:T(1,128)S(1)}, u32[]{:S(2)}, u32[]{:S(2)}) async-start(f32[256,1,128]{2,1,0:T(1,128)} %bitcast.1), calls=%async_computation.6 | async-start | bytes 262144 | tf_op jit(solution)/shard_map/all_to_all | solution.py:472
  221.2 5.8 %collective-permute-start.26 = (f32[136,256]{1,0:T(8,128)S(1)}, f32[136,256]{1,0:T(8,128)S(1)}, u32[]{:S(2)}, u32[]{:S(2)}) collective-permute-start(f32[136,256]{1,0:T(8,128)S(1)} %get-tuple-element.86.c0.n0), channel_id=1, source_target_pairs={{0,1},{1,2},{2,3},{3,0},{4,5},{5,6},{6,7},{7,4},{8,9},{9,10},{10,1... | collective-permute-start | bytes 417800 | tf_op jit(solution)/shard_map/ppermute | solution.py:41
  222.6 10.0 %collective-permute-start.25 = (f32[136,256]{1,0:T(8,128)S(1)}, f32[136,256]{1,0:T(8,128)S(1)}, u32[]{:S(2)}, u32[]{:S(2)}) collective-permute-start(f32[136,256]{1,0:T(8,128)S(1)} %get-tuple-element.86.c0.n0), channel_id=1, source_target_pairs={{0,2},{1,3},{2,0},{3,1},{4,6},{5,7},{6,4},{7,5},{8,10},{9,11},{10,... | collective-permute-start | bytes 417800 | tf_op jit(solution)/shard_map/ppermute | solution.py:41
  225.0 7.6 %collective-permute-start.24 = (f32[136,256]{1,0:T(8,128)S(1)}, f32[136,256]{1,0:T(8,128)S(1)}, u32[]{:S(2)}, u32[]{:S(2)}) collective-permute-start(f32[136,256]{1,0:T(8,128)S(1)} %get-tuple-element.86.c0.n0), channel_id=1, source_target_pairs={{0,3},{1,0},{2,1},{3,2},{4,7},{5,4},{6,5},{7,6},{8,11},{9,8},{10,9... | collective-permute-start | bytes 417800 | tf_op jit(solution)/shard_map/ppermute | solution.py:41
